TPU v7x, 256 devices: a whole 4x4x8 slice. The times are simulated.
256 devices in a mesh: gx: 4 (over x), gy: 4 (over z_hi), gz: 16 (over y, z_lo, core).
Axes of the slice: x: 4, y: 4, z: 8 (z_hi: 4, z_lo: 2; z = z_hi * 2 + z_lo), core: 2. Of those that a mesh axis runs over, the one named last changes fastest.
Arguments:
- density: float32 [32, 256, 2048], P('gx', 'gy', 'gz'), may hold values from 0.2 to 6, as said below
- momentum: float32 [3, 32, 256, 2048], P(None, 'gx', 'gy', 'gz'), may hold values from -6 to 6
- energy: float32 [32, 256, 2048], P('gx', 'gy', 'gz'), may hold values from 0.2 to 6, as said below
- displacement: int32 [3, 32, 256, 2048], P(None, 'gx', 'gy', 'gz'), may hold values from -255 to 255
- flags: int32 [6], replicated, may hold values from 0 to 1
Outputs:
- new_density: float32 [32, 256, 2048], P('gx', 'gy', 'gz')
- new_momentum: float32 [3, 32, 256, 2048], P(None, 'gx', 'gy', 'gz')
- new_energy: float32 [32, 256, 2048], P('gx', 'gy', 'gz')
- totals: float32 [2], replicated
Inputs may be any that keep to these rules, and one draw needn't show every extreme that they name: density is positive. energy is positive.
All inputs are finite; a program needn't handle non-finite values.
Results may differ from a plain program's by a relative error of at most 0.0003.
Values sent between devices are 32-bit elements; how exact they have to be, the bound alone decides.
A program may use at most 64 MiB of HBM per device.

v0:
```python
import jax
import jax.numpy as jnp
from jax import lax
from jax.sharding import Mesh
from jax.sharding import PartitionSpec as P

GZ = ("gz_0", "gz_1", "gz_2")
GX_GY_GZ = ("gx", "gy", "gz_0", "gz_1", "gz_2")


def one_axis_at_a_time(shard, axes):
    for axis in axes:
        shard = lax.psum(shard, axis)
    return shard


def from_behind(value, axis, steps):
    count = lax.axis_size(axis)
    leading, last = (max(0, -steps), min(count, count - steps))
    return lax.ppermute(value, axis, [(source, source + steps) for source in range(leading, last)])


def extended(shard, sides, width):
    edges = {}
    for axis, dim in sides:
        peers, length = (lax.axis_size(axis), shard.shape[dim])
        up = [(i, (i + 1) % peers) for i in range(peers - 1)]
        last = lax.slice_in_dim(shard, length - width, length, axis=dim)
        leading = lax.slice_in_dim(shard, 0, width, axis=dim)
        edges[dim] = (
            lax.ppermute(last, axis, up),
            lax.ppermute(leading, axis, [(b, a) for a, b in up]),
        )
    done = []
    for _, dim in sides:
        low, high = edges[dim]
        around = [(width, width) if d in done else (0, 0) for d in range(shard.ndim)]
        shard = jnp.concatenate([jnp.pad(low, around), shard, jnp.pad(high, around)], axis=dim)
        done.append(dim)
    return shard


def minmod(left_diff, right_diff):
    return (
        0.5
        * (jnp.sign(left_diff) + jnp.sign(right_diff))
        * jnp.minimum(jnp.abs(left_diff), jnp.abs(right_diff))
    )


def flux_change(padded, face_rows, along):
    total_len = padded.shape[along]
    upper_cells = lax.slice_in_dim(padded, 2, total_len, axis=along)
    middle = lax.slice_in_dim(padded, 1, total_len - 1, axis=along)
    lower_cells = lax.slice_in_dim(padded, 0, total_len - 2, axis=along)
    slopes = minmod(upper_cells - middle, middle - lower_cells)
    k = total_len - 2
    low_val = lax.slice_in_dim(middle, 0, k - 1, axis=along)
    high_val = lax.slice_in_dim(middle, 1, k, axis=along)
    low_slope = lax.slice_in_dim(slopes, 0, k - 1, axis=along)
    high_slope = lax.slice_in_dim(slopes, 1, k, axis=along)
    fluxes = face_rows * jnp.where(
        face_rows > 0,
        low_val + 0.5 * (1.0 - face_rows) * low_slope,
        high_val - 0.5 * (1.0 + face_rows) * high_slope,
    )
    m = k - 1
    return lax.slice_in_dim(fluxes, 0, m - 1, axis=along) - lax.slice_in_dim(
        fluxes, 1, m, axis=along
    )


def fix_ghosts(padded, along, position, count_on):
    total_len = padded.shape[along]
    first_cell = lax.slice_in_dim(padded, 2, 3, axis=along)
    last_cell = lax.slice_in_dim(padded, total_len - 3, total_len - 2, axis=along)
    low_ghosts = jnp.where(
        position == 0,
        jnp.concatenate([first_cell, first_cell], along),
        lax.slice_in_dim(padded, 0, 2, axis=along),
    )
    high_ghosts = jnp.where(
        position == count_on - 1,
        jnp.concatenate([last_cell, last_cell], along),
        lax.slice_in_dim(padded, total_len - 2, total_len, axis=along),
    )
    return jnp.concatenate(
        [low_ghosts, lax.slice_in_dim(padded, 2, total_len - 2, axis=along), high_ghosts], along
    )


def face_edges(face_speed, comp, position, flag_open):
    n = face_speed.shape[comp]
    low_face = lax.slice_in_dim(face_speed, 0, 1, axis=comp) * jnp.where(
        position == 0, flag_open[2 * comp], 1.0
    )
    last_face = lax.slice_in_dim(face_speed, n - 1, n, axis=comp) * flag_open[2 * comp + 1]
    return (low_face, last_face)


def face_build(face_speed, comp, next_plane, position, count_on, flag_open):
    n = face_speed.shape[comp]
    low_face, last_face = face_edges(face_speed, comp, position, flag_open)
    high_face = jnp.where(
        position == count_on - 1, last_face, next_plane.astype(jnp.float32) / 256.0
    )
    face_rows = jnp.concatenate(
        [low_face, lax.slice_in_dim(face_speed, 1, n, axis=comp), high_face], comp
    )
    return face_rows[None]


def boundary_gain(conserved, face_speed, comp, position, count_on, flag_open):
    n = conserved.shape[comp + 1]
    low_face, last_face = face_edges(face_speed, comp, position, flag_open)
    first_cell = lax.slice_in_dim(conserved, 0, 1, axis=comp + 1)
    last_cell = lax.slice_in_dim(conserved, n - 1, n, axis=comp + 1)
    reduce_dims = (1, 2, 3)
    gain_in = jnp.where(position == 0, jnp.sum(first_cell * low_face[None], axis=reduce_dims), 0.0)
    gain_out = jnp.where(
        position == count_on - 1, jnp.sum(last_cell * last_face[None], axis=reduce_dims), 0.0
    )
    return gain_in - gain_out


def shards(density, momentum, energy, displacement, flags):
    fields = jnp.concatenate([density[None], momentum, energy[None]], 0)
    face_speed = displacement.astype(jnp.float32) / 256.0
    flag_open = flags.astype(jnp.float32)
    pos_x, pos_y, pos_z = (lax.axis_index("gx"), lax.axis_index("gy"), lax.axis_index(GZ))
    size_x, size_y, size_z = (lax.axis_size("gx"), lax.axis_size("gy"), lax.axis_size(GZ))
    cell_total = float(
        fields.shape[1] * fields.shape[2] * fields.shape[3] * size_x * size_y * size_z
    )
    conserved = fields[0::4]
    start_sum = jnp.sum(conserved, axis=(1, 2, 3))
    start_sum = start_sum + boundary_gain(conserved, face_speed[0], 0, pos_x, size_x, flag_open)
    start_sum = start_sum + boundary_gain(conserved, face_speed[1], 1, pos_y, size_y, flag_open)
    start_sum = start_sum + boundary_gain(conserved, face_speed[2], 2, pos_z, size_z, flag_open)
    mass_sum, energy_sum = (
        one_axis_at_a_time(start_sum[0], GX_GY_GZ),
        one_axis_at_a_time(start_sum[1], GX_GY_GZ),
    )
    next_xplane = from_behind(displacement[0, 0:1], "gx", -1)
    next_yplane = from_behind(displacement[1, :, 0:1], "gy", -1)
    next_zplane = from_behind(displacement[2, :, :, 0:1], GZ, -1)
    faces_x = face_build(face_speed[0], 0, next_xplane, pos_x, size_x, flag_open)
    faces_y = face_build(face_speed[1], 1, next_yplane, pos_y, size_y, flag_open)
    faces_z = face_build(face_speed[2], 2, next_zplane, pos_z, size_z, flag_open)
    padded = extended(fields, (("gx", 1), ("gy", 2), (GZ, 3)), 2)
    along_x = padded[:, :, 2:-2, 2:-2]
    along_y = padded[:, 2:-2, :, 2:-2]
    along_z = padded[:, 2:-2, 2:-2, :]
    updated = fields + flux_change(fix_ghosts(along_x, 1, pos_x, size_x), faces_x, 1)
    updated = updated + flux_change(fix_ghosts(along_y, 2, pos_y, size_y), faces_y, 2)
    updated = updated + flux_change(fix_ghosts(along_z, 3, pos_z, size_z), faces_z, 3)
    totals = jnp.stack([mass_sum, energy_sum]) / cell_total
    return (updated[0], updated[1:4], updated[4], totals)


def solution(mesh):
    finer = Mesh(
        mesh.devices.reshape(mesh.shape["gx"], mesh.shape["gy"], 4, 2, 2),
        ("gx", "gy", "gz_0", "gz_1", "gz_2"),
    )
    return jax.shard_map(
        shards,
        mesh=finer,
        in_specs=(
            P("gx", "gy", GZ),
            P(None, "gx", "gy", GZ),
            P("gx", "gy", GZ),
            P(None, "gx", "gy", GZ),
            P(),
        ),
        out_specs=(P("gx", "gy", GZ), P(None, "gx", "gy", GZ), P("gx", "gy", GZ), P()),
        check_vma=False,
    )
```

profile of v0, /device:TPU:5, one launch (start us, length us, event | category | flops | bytes accessed | tf_op | source)
XLA Modules:
  0.0 131.2 jit_solution(6480736132568746061)
XLA Ops:
  2.0 1.5 %fusion.37 = (f32[5,8,64,2]{3,2,1,0:T(8,128)}, f32[5,8,64,2]{3,2,1,0:T(8,128)S(1)}) fusion(f32[5,8,64,128]{3,2,1,0:T(8,128)S(1)} %pad_maximum_fusion.15), kind=kLoop, calls=%fused_computation.117 | loop fusion | bytes 81920 | tf_op jit(solution)/shard_map/slice | solution.py:28
  3.5 2.4 %copy.159 = f32[5,8,64,2]{2,1,3,0:T(8,128)} copy(f32[5,8,64,2]{3,2,1,0:T(8,128)} %get-tuple-element.50) | data formatting | bytes 40960 | tf_op jit(solution)/shard_map/slice | solution.py:28
  5.9 4.1 %collective-permute-start.7 = (f32[5,8,64,2]{2,1,3,0:T(8,128)}, f32[5,8,64,2]{2,1,3,0:T(8,128)}, u32[]{:S(2)}, u32[]{:S(2)}) collective-permute-start(f32[5,8,64,2]{2,1,3,0:T(8,128)} %copy.159), channel_id=1, source_target_pairs={{0,1},{1,2},{2,3},{3,4},{4,5},{5,6},{6,7},{7,8},{8,9},{9,10},{10,1... | collective-permute-start | bytes 61448 | tf_op jit(solution)/shard_map/ppermute | solution.py:31
  11.1 1.9 %collective-permute-start.8 = (f32[5,8,64,2]{2,1,3,0:T(8,128)}, f32[5,8,64,2]{2,1,3,0:T(8,128)}, u32[]{:S(2)}, u32[]{:S(2)}) collective-permute-start(f32[5,8,64,2]{2,1,3,0:T(8,128)} %copy.161), channel_id=1, source_target_pairs={{1,0},{2,1},{3,2},{4,3},{5,4},{6,5},{7,6},{8,7},{9,8},{10,9},{11,1... | collective-permute-start | bytes 61448 | tf_op jit(solution)/shard_map/ppermute | solution.py:32
  15.0 1.9 %collective-permute-start.6 = (s32[8,64,1]{2,1,0:T(8,128)}, s32[8,64,1]{2,1,0:T(8,128)}, u32[]{:S(2)}, u32[]{:S(2)}) collective-permute-start(s32[8,64,1]{2,1,0:T(8,128)} %copy.158), channel_id=1, source_target_pairs={{1,0},{2,1},{3,2},{4,3},{5,4},{6,5},{7,6},{8,7},{9,8},{10,9},{11,1... | collective-permute-start | bytes 6152 | tf_op jit(solution)/shard_map/ppermute | solution.py:20
  17.5 5.5 %collective-permute-start.4 = (f32[5,8,2,128]{3,1,2,0:T(8,128)}, f32[5,8,2,128]{3,1,2,0:T(8,128)}, u32[]{:S(2)}, u32[]{:S(2)}) collective-permute-start(f32[5,8,2,128]{3,1,2,0:T(8,128)} %copy.153), channel_id=1, source_target_pairs={{0,16},{16,32},{32,48},{1,17},{17,33},{33,49},{2,18},{18,34},{34,5... | collective-permute-start | bytes 122888 | tf_op jit(solution)/shard_map/ppermute | solution.py:31
  25.1 1.9 %fusion.36 = (f32[5,8,64,1]{3,2,1,0:T(8,128)}, f32[5,8,64,1]{3,2,1,0:T(8,128)}) fusion(f32[5,8,64,128]{3,2,1,0:T(8,128)S(1)} %pad_maximum_fusion.15), kind=kLoop, calls=%fused_computation.116 | loop fusion | bytes 40960 | tf_op jit(solution)/shard_map/slice | solution.py:75
  35.7 1.8 %fusion.17 = (f32[8,64]{1,0:T(8,128)S(1)}, f32[8,64,1]{2,1,0:T(8,128)S(1)}, f32[8,64]{1,0:T(8,128)S(1)}, f32[8,64,1]{2,1,0:T(8,128)S(1)}) fusion(f32[8,64,128]{2,1,0:T(8,128)S(1)} %get-tuple-element.56, f32[]{:T(128)} %bitcast.15, s32[8,64,1]{2,1,0:T(8,128)} %collective-permute-done.6, pred[]{:T(512)S(6)} %eq.17, f32[]{:T(128)S(6)} %select_n.145), kind=kLoop, calls=%fused_computation.72 | loop fusion | flops 2560 | bytes 14345 | tf_op jit(solution)/shard_map/mul | solution.py:97
  40.6 2.8 %collective-permute-start.1 = (f32[5,2,64,128]{3,2,1,0:T(8,128)}, f32[5,2,64,128]{3,2,1,0:T(8,128)}, u32[]{:S(2)}, u32[]{:S(2)}) collective-permute-start(f32[5,2,64,128]{3,2,1,0:T(8,128)} %get-tuple-element.42), channel_id=1, source_target_pairs={{0,64},{64,128},{128,192},{1,65},{65,129},{129,193},{2,66},{66,130... | collective-permute-start | bytes 983048 | tf_op jit(solution)/shard_map/ppermute | solution.py:31
  47.3 7.0 %all-reduce.2 = (f32[]{:T(128)}, f32[]{:T(128)}) all-reduce(f32[]{:T(128)} %bitcast.25, f32[]{:T(128)} %bitcast.23), channel_id=1, replica_groups=mesh['gx'=4,'gy'=4,'gz_0'=4,'gz_1'=2,'gz_2'=2] {'gx'}, use_global_device_ids=true, to_apply=%region_12.13 | all-reduce | flops 2 | bytes 16 | tf_op jit(solution)/shard_map/psum | solution.py:13
  54.2 14.2 %all-reduce.1 = (f32[]{:T(128)}, f32[]{:T(128)}) all-reduce(f32[]{:T(128)} %get-tuple-element.18, f32[]{:T(128)} %get-tuple-element.19), channel_id=1, replica_groups=mesh['gx'=4,'gy'=4,'gz_0'=4,'gz_1'=2,'gz_2'=2] {'gy'}, use_global_device_ids=true, to_apply=%region_13.14 | all-reduce | flops 2 | bytes 16 | tf_op jit(solution)/shard_map/psum | solution.py:13
  68.4 10.9 %all-reduce = (f32[]{:T(128)}, f32[]{:T(128)}) all-reduce(f32[]{:T(128)} %get-tuple-element.16, f32[]{:T(128)} %get-tuple-element.17), channel_id=1, replica_groups=mesh['gx'=4,'gy'=4,'gz_0'=4,'gz_1'=2,'gz_2'=2] {'gz_0'}, use_global_device_ids=true, to_apply=%region_14.15 | all-reduce | flops 2 | bytes 16 | tf_op jit(solution)/shard_map/psum | solution.py:13
  79.3 4.4 %all-reduce.4 = (f32[]{:T(128)}, f32[]{:T(128)}) all-reduce(f32[]{:T(128)} %get-tuple-element.14, f32[]{:T(128)} %get-tuple-element.15), channel_id=1, replica_groups=mesh['gx'=4,'gy'=4,'gz_0'=4,'gz_1'=2,'gz_2'=2] {'gz_1'}, use_global_device_ids=true, to_apply=%region_15.16 | all-reduce | flops 2 | bytes 16 | tf_op jit(solution)/shard_map/psum | solution.py:13
  83.7 10.6 %all-reduce.3 = (f32[1]{0:T(128)}, f32[1]{0:T(128)}) all-reduce(f32[1]{0:T(128)} %bitcast.26, f32[1]{0:T(128)} %bitcast.24), channel_id=1, replica_groups=mesh['gx'=4,'gy'=4,'gz_0'=4,'gz_1'=2,'gz_2'=2] {'gz_2'}, use_global_device_ids=true, to_apply=%region_16.17 | all-reduce | flops 2 | bytes 16 | tf_op jit(solution)/shard_map/psum | solution.py:13
  94.4 1.7 %maximum_multiply_fusion = f32[2]{0:T(128)} fusion(f32[1]{0:T(128)} %get-tuple-element.20, f32[1]{0:T(128)} %get-tuple-element.21), kind=kLoop, calls=%fused_computation.109 | loop fusion | flops 4 | bytes 16 | tf_op jit(solution)/shard_map/div | solution.py:157
  96.1 4.1 %collective-permute-start.2 = (f32[5,2,64,128]{3,2,1,0:T(8,128)}, f32[5,2,64,128]{3,2,1,0:T(8,128)}, u32[]{:S(2)}, u32[]{:S(2)}) collective-permute-start(f32[5,2,64,128]{3,2,1,0:T(8,128)} %get-tuple-element.43), channel_id=1, source_target_pairs={{64,0},{128,64},{192,128},{65,1},{129,65},{193,129},{66,2},{130,66... | collective-permute-start | bytes 983048 | tf_op jit(solution)/shard_map/ppermute | solution.py:32
  100.1 2.3 %copy.162 = f32[5,8,64,2]{3,2,1,0:T(8,128)} copy(f32[5,8,64,2]{2,1,3,0:T(8,128)} %collective-permute-done.8) | data formatting | bytes 40960 | tf_op jit(solution)/shard_map/ppermute | solution.py:32
  102.5 2.6 %maximum_select_fusion.1 = f32[5,8,64,2]{3,2,1,0:T(8,128)S(1)} fusion(f32[5,8,64,2]{3,2,1,0:T(8,128)} %copy.162, f32[5,8,64,1]{3,2,1,0:T(8,128)} %get-tuple-element.49, pred[]{:T(512)S(6)} %eq.17), kind=kLoop, calls=%fused_computation.47 | loop fusion | flops 10240 | bytes 51201 | tf_op jit(solution)/shard_map/jit(_where)/select_n | solution.py:82
  105.1 1.7 %pad_maximum_fusion.4 = f32[5,8,64,130]{3,2,1,0:T(8,128)} fusion(f32[5,8,64,2]{3,2,1,0:T(8,128)S(1)} %maximum_select_fusion.1, f32[1,8,64,128]{3,2,1,0:T(8,128)S(1)} %bitcast.42, f32[3,8,64,128]{3,2,1,0:T(8,128)S(1)} %copy-done, f32[1,8,64,128]{3,2,1,0:T(8,128)S(1)} %bitcast.50), kind=kLoop, calls=%fused_computation.11 | loop fusion | flops 998400 | bytes 2662400 | tf_op jit(solution)/shard_map/concatenate | solution.py:87
  106.9 2.6 %collective-permute-start = (s32[1,64,128]{2,1,0:T(8,128)}, s32[1,64,128]{2,1,0:T(8,128)}, u32[]{:S(2)}, u32[]{:S(2)}) collective-permute-start(s32[1,64,128]{2,1,0:T(8,128)} %slice_bitcast_fusion.5), channel_id=1, source_target_pairs={{64,0},{128,64},{192,128},{65,1},{129,65},{193,129},{66,2},{130,66... | collective-permute-start | bytes 98312 | tf_op jit(solution)/shard_map/ppermute | solution.py:20
  109.5 2.3 %copy.160 = f32[5,8,64,2]{3,2,1,0:T(8,128)} copy(f32[5,8,64,2]{2,1,3,0:T(8,128)} %collective-permute-done.7) | data formatting | bytes 40960 | tf_op jit(solution)/shard_map/ppermute | solution.py:31
  111.8 2.5 %maximum_select_fusion = f32[5,8,64,2]{3,2,1,0:T(8,128)S(1)} fusion(f32[5,8,64,2]{3,2,1,0:T(8,128)} %copy.160, f32[5,8,64,1]{3,2,1,0:T(8,128)} %get-tuple-element.48, pred[]{:T(512)S(6)} %eq.16), kind=kLoop, calls=%fused_computation.46 | loop fusion | flops 10240 | bytes 51201 | tf_op jit(solution)/shard_map/jit(_where)/select_n | solution.py:77
  114.3 3.1 %maximum_maximum_fusion = (f32[5,8,64,130]{3,2,1,0:T(8,128)S(1)}, f32[5,8,64,130]{3,2,1,0:T(8,128)S(1)}) fusion(f32[1,8,64,128]{3,2,1,0:T(8,128)S(1)} %bitcast.43, f32[3,8,64,128]{3,2,1,0:T(8,128)S(1)} %copy-done, f32[1,8,64,128]{3,2,1,0:T(8,128)S(1)} %bitcast.51, f32[5,8,64,2]{3,2,1,0:T(8,128)S(1)} %maximum_select_fusion, ...), kind=kLoop, calls=%fused_computation.10 | loop fusion | flops 6656000 | bytes 4014080 | tf_op jit(solution)/shard_map/concatenate | solution.py:87
  117.5 1.4 %fusion.2 = f32[5,8,64,129]{3,2,1,0:T(8,128)S(1)} fusion(f32[5,8,64,130]{3,2,1,0:T(8,128)S(1)} %get-tuple-element.31, f32[5,8,64,130]{3,2,1,0:T(8,128)S(1)} %copy-done.3, f32[5,8,64,130]{3,2,1,0:T(8,128)S(1)} %get-tuple-element.30, f32[8,64,129]{2,1,0:T(8,128)S(1)} %copy-done.6, f32[8,64,129]{2,1,0:T(8,128)S(1)} %copy-done.5, ...), kind=kLoop, calls=%fused_computation.3 | loop fusion | flops 1981440 | bytes 7463424 | tf_op jit(solution)/shard_map/mul | solution.py:62
  (97 shorter events, 32.8 us)
Async XLA Ops:
  5.9 101.0 %collective-permute-start.7 = (f32[5,8,64,2]{2,1,3,0:T(8,128)}, f32[5,8,64,2]{2,1,3,0:T(8,128)}, u32[]{:S(2)}, u32[]{:S(2)}) collective-permute-start(f32[5,8,64,2]{2,1,3,0:T(8,128)} %copy.159), channel_id=1, source_target_pairs={{0,1},{1,2},{2,3},{3,4},{4,5},{5,6},{6,7},{7,8},{8,9},{9,10},{10,1... | collective-permute-start | bytes 61448 | tf_op jit(solution)/shard_map/ppermute | solution.py:31
  11.1 85.0 %collective-permute-start.8 = (f32[5,8,64,2]{2,1,3,0:T(8,128)}, f32[5,8,64,2]{2,1,3,0:T(8,128)}, u32[]{:S(2)}, u32[]{:S(2)}) collective-permute-start(f32[5,8,64,2]{2,1,3,0:T(8,128)} %copy.161), channel_id=1, source_target_pairs={{1,0},{2,1},{3,2},{4,3},{5,4},{6,5},{7,6},{8,7},{9,8},{10,9},{11,1... | collective-permute-start | bytes 61448 | tf_op jit(solution)/shard_map/ppermute | solution.py:32
  15.0 19.4 %collective-permute-start.6 = (s32[8,64,1]{2,1,0:T(8,128)}, s32[8,64,1]{2,1,0:T(8,128)}, u32[]{:S(2)}, u32[]{:S(2)}) collective-permute-start(s32[8,64,1]{2,1,0:T(8,128)} %copy.158), channel_id=1, source_target_pairs={{1,0},{2,1},{3,2},{4,3},{5,4},{6,5},{7,6},{8,7},{9,8},{10,9},{11,1... | collective-permute-start | bytes 6152 | tf_op jit(solution)/shard_map/ppermute | solution.py:20
  17.5 103.9 %collective-permute-start.4 = (f32[5,8,2,128]{3,1,2,0:T(8,128)}, f32[5,8,2,128]{3,1,2,0:T(8,128)}, u32[]{:S(2)}, u32[]{:S(2)}) collective-permute-start(f32[5,8,2,128]{3,1,2,0:T(8,128)} %copy.153), channel_id=1, source_target_pairs={{0,16},{16,32},{32,48},{1,17},{17,33},{33,49},{2,18},{18,34},{34,5... | collective-permute-start | bytes 122888 | tf_op jit(solution)/shard_map/ppermute | solution.py:31
  23.6 3.4 %copy-start.7 = (s32[3,8,64,128]{3,2,1,0:T(8,128)S(1)}, s32[3,8,64,128]{3,2,1,0:T(8,128)}, u32[]{:S(2)}) copy-start(s32[3,8,64,128]{3,2,1,0:T(8,128)} %param.8) | copy-start | bytes 2359300
  23.6 96.8 %collective-permute-start.5 = (f32[5,8,2,128]{3,1,2,0:T(8,128)}, f32[5,8,2,128]{3,1,2,0:T(8,128)}, u32[]{:S(2)}, u32[]{:S(2)}) collective-permute-start(f32[5,8,2,128]{3,1,2,0:T(8,128)} %copy.155), channel_id=1, source_target_pairs={{16,0},{32,16},{48,32},{17,1},{33,17},{49,33},{18,2},{34,18},{50,3... | collective-permute-start | bytes 122888 | tf_op jit(solution)/shard_map/ppermute | solution.py:32
  27.1 4.5 %copy-start.4 = (f32[3,8,64,128]{3,2,1,0:T(8,128)}, f32[3,8,64,128]{3,2,1,0:T(8,128)S(1)}, u32[]{:S(2)}) copy-start(f32[3,8,64,128]{3,2,1,0:T(8,128)S(1)} %convert_multiply_fusion) | copy-start | bytes 2359300
  30.1 3.1 %copy-start.11 = (f32[8,64,128]{2,1,0:T(8,128)}, f32[8,64,128]{2,1,0:T(8,128)S(1)}, u32[]{:S(2)}) copy-start(f32[8,64,128]{2,1,0:T(8,128)S(1)} %get-tuple-element.55) | copy-start | bytes 786436
  34.4 6.2 %collective-permute-start.3 = (s32[8,1,128]{2,1,0:T(1,128)S(1)}, s32[8,1,128]{2,1,0:T(1,128)S(1)}, u32[]{:S(2)}, u32[]{:S(2)}) collective-permute-start(s32[8,1,128]{2,1,0:T(1,128)S(1)} %slice_bitcast_fusion.6), channel_id=1, source_target_pairs={{16,0},{32,16},{48,32},{17,1},{33,17},{49,33},{18,2},{34,18},{50,3... | collective-permute-start | bytes 12296 | tf_op jit(solution)/shard_map/ppermute | solution.py:20
  40.6 85.1 %collective-permute-start.1 = (f32[5,2,64,128]{3,2,1,0:T(8,128)}, f32[5,2,64,128]{3,2,1,0:T(8,128)}, u32[]{:S(2)}, u32[]{:S(2)}) collective-permute-start(f32[5,2,64,128]{3,2,1,0:T(8,128)} %get-tuple-element.42), channel_id=1, source_target_pairs={{0,64},{64,128},{128,192},{1,65},{65,129},{129,193},{2,66},{66,130... | collective-permute-start | bytes 983048 | tf_op jit(solution)/shard_map/ppermute | solution.py:31
  96.1 28.2 %collective-permute-start.2 = (f32[5,2,64,128]{3,2,1,0:T(8,128)}, f32[5,2,64,128]{3,2,1,0:T(8,128)}, u32[]{:S(2)}, u32[]{:S(2)}) collective-permute-start(f32[5,2,64,128]{3,2,1,0:T(8,128)} %get-tuple-element.43), channel_id=1, source_target_pairs={{64,0},{128,64},{192,128},{65,1},{129,65},{193,129},{66,2},{130,66... | collective-permute-start | bytes 983048 | tf_op jit(solution)/shard_map/ppermute | solution.py:32
  102.5 2.6 %copy-start = (f32[3,8,64,128]{3,2,1,0:T(8,128)S(1)}, f32[3,8,64,128]{3,2,1,0:T(8,128)}, u32[]{:S(2)}) copy-start(f32[3,8,64,128]{3,2,1,0:T(8,128)} %param.6) | copy-start | bytes 2359300
  102.5 2.6 %copy-start.1 = (f32[8,64,128]{2,1,0:T(8,128)S(1)}, f32[8,64,128]{2,1,0:T(8,128)}, u32[]{:S(2)}) copy-start(f32[8,64,128]{2,1,0:T(8,128)} %param.7) | copy-start | bytes 786436
  102.5 2.6 %copy-start.2 = (f32[8,64,128]{2,1,0:T(8,128)S(1)}, f32[8,64,128]{2,1,0:T(8,128)}, u32[]{:S(2)}) copy-start(f32[8,64,128]{2,1,0:T(8,128)} %param.5) | copy-start | bytes 786436
  106.9 12.0 %collective-permute-start = (s32[1,64,128]{2,1,0:T(8,128)}, s32[1,64,128]{2,1,0:T(8,128)}, u32[]{:S(2)}, u32[]{:S(2)}) collective-permute-start(s32[1,64,128]{2,1,0:T(8,128)} %slice_bitcast_fusion.5), channel_id=1, source_target_pairs={{64,0},{128,64},{192,128},{65,1},{129,65},{193,129},{66,2},{130,66... | collective-permute-start | bytes 98312 | tf_op jit(solution)/shard_map/ppermute | solution.py:20
  114.3 3.1 %copy-start.3 = (f32[5,8,64,130]{3,2,1,0:T(8,128)S(1)}, f32[5,8,64,130]{3,2,1,0:T(8,128)}, u32[]{:S(2)}) copy-start(f32[5,8,64,130]{3,2,1,0:T(8,128)} %pad_maximum_fusion.4) | copy-start | bytes 3993604
  114.3 3.1 %copy-start.5 = (f32[8,64,129]{2,1,0:T(8,128)S(1)}, f32[8,64,129]{2,1,0:T(8,128)}, u32[]{:S(2)}) copy-start(f32[8,64,129]{2,1,0:T(8,128)} %get-tuple-element.57) | copy-start | bytes 792580
  114.3 3.1 %copy-start.6 = (f32[8,64,129]{2,1,0:T(8,128)S(1)}, f32[8,64,129]{2,1,0:T(8,128)}, u32[]{:S(2)}) copy-start(f32[8,64,129]{2,1,0:T(8,128)} %get-tuple-element.58) | copy-start | bytes 792580
  114.3 3.1 %copy-start.13 = (pred[8,64,129]{2,1,0:T(8,128)(4,1)S(1)}, pred[8,64,129]{2,1,0:T(8,128)(4,1)}, u32[]{:S(2)}) copy-start(pred[8,64,129]{2,1,0:T(8,128)(4,1)} %get-tuple-element.28) | copy-start | bytes 198148
  117.5 2.9 %copy-start.15 = (f32[1,64,128]{2,1,0:T(8,128)S(1)}, f32[1,64,128]{2,1,0:T(8,128)}, u32[]{:S(2)}) copy-start(f32[1,64,128]{2,1,0:T(8,128)} %get-tuple-element.54) | copy-start | bytes 98308
  118.9 1.6 %copy-start.17 = (f32[5,8,1,128]{3,2,1,0:T(1,128)S(1)}, f32[5,8,1,128]{3,2,1,0:T(1,128)}, u32[]{:S(2)}) copy-start(f32[5,8,1,128]{3,2,1,0:T(1,128)} %get-tuple-element.47) | copy-start | bytes 61444
  122.3 1.3 %copy-start.8 = (f32[8,65,128]{2,1,0:T(8,128)S(1)}, f32[8,65,128]{2,1,0:T(8,128)}, u32[]{:S(2)}) copy-start(f32[8,65,128]{2,1,0:T(8,128)} %get-tuple-element.62) | copy-start | bytes 798724
  122.3 1.3 %copy-start.9 = (f32[8,65,128]{2,1,0:T(8,128)S(1)}, f32[8,65,128]{2,1,0:T(8,128)}, u32[]{:S(2)}) copy-start(f32[8,65,128]{2,1,0:T(8,128)} %get-tuple-element.63) | copy-start | bytes 798724
  122.3 1.3 %copy-start.10 = (f32[8,65,128]{2,1,0:T(8,128)S(1)}, f32[8,65,128]{2,1,0:T(8,128)}, u32[]{:S(2)}) copy-start(f32[8,65,128]{2,1,0:T(8,128)} %get-tuple-element.64) | copy-start | bytes 798724
  (4 other events, 4.2 us)
where the time goes:
time: 132 us; the launch traced here: 131 us
  blocking collectives  47.1 us (36%)
  other arithmetic  33.4 us (25%)
  starting transfers between devices  25.6 us (19%)
  local copies, waits for them, and re-layouts  21.4 us (16%)
  between operations  3.05 us (2%)
    psum x5, blocking collectives, one_axis_at_a_time(): shard = lax.psum(shard, axis)  47.1 us
    ppermute x3, starting transfers between devices, extended(): lax.ppermute(last, axis, up)  12.4 us
    concatenate x6, other arithmetic, fix_ghosts(): jnp.concatenate([low_ghosts, lax.slice_in_dim(padded, 2, total_len - 2, a...  7.63 us
    ppermute x3, starting transfers between devices, extended(): lax.ppermute(leading, axis, [(b, a) for a, b in up])  7.41 us
    ppermute x3, starting transfers between devices, from_behind(): lax.ppermute(value, axis, [(source, source + steps) for source in range(l...  5.77 us
    slice x5, local copies, waits for them, and re-layouts, extended(): last = lax.slice_in_dim(shard, length - width, length, axis=dim)  5.46 us
    select_n x3, other arithmetic, fix_ghosts(): jnp.where(position == count_on - 1, jnp.concatenate([last_cell, last_cell...  4.44 us
    select_n x3, other arithmetic, fix_ghosts(): jnp.where(position == 0, jnp.concatenate([first_cell, first_cell], along)...  4.35 us
  transfers between devices with their start and end apart: 9, of which 1 were waited for; matrix products, arithmetic and copies ran while one was open for 33% of the time, Pallas kernels for 0%

commit v1 on v0

v1 whole, which is shorter than its diff:
```python
import functools

import jax
import jax.numpy as jnp
from jax import lax
from jax.experimental import pallas as pl
from jax.experimental.pallas import tpu as pltpu
from jax.sharding import PartitionSpec as P

MESH = pl.DeviceIdType.MESH
STEP = 1.0 / 256.0


def minmod(left_diff, right_diff):
    least = jnp.minimum(left_diff, right_diff)
    most = jnp.maximum(left_diff, right_diff)
    return jnp.maximum(least, jnp.minimum(most, 0.0))


def half_weight(v):
    size = jnp.abs(v)
    return 0.5 * size * (1.0 - size)


def shift_down(block, first_row):
    moved = pltpu.roll(block, 1, 0)
    row = lax.broadcasted_iota(jnp.int32, (8, 128), 0)
    top = jnp.where(row == 0, first_row, moved[:8])
    return jnp.concatenate([top, moved[8:]], 0)


def shift_up(block, last_row):
    n = block.shape[0]
    moved = pltpu.roll(block, n - 1, 0)
    row = lax.broadcasted_iota(jnp.int32, (8, 128), 0)
    bottom = jnp.where(row == 7, last_row, moved[n - 8 :])
    return jnp.concatenate([moved[: n - 8], bottom], 0)


def back(block):
    return pltpu.roll(block, 1, 1)


def ahead(block):
    return pltpu.roll(block, 127, 1)


def kernel(
    cells,
    density,
    momentum,
    energy,
    displacement,
    flags,
    new_density,
    new_momentum,
    new_energy,
    totals,
    q,
    disp,
    flag,
    acc,
    vx,
    gx_w,
    xlow,
    xhigh,
    xface,
    yup,
    ydown,
    ylow,
    yhigh,
    yedge,
    zpack,
    zlow,
    zhigh,
    zslope,
    zflow,
    zface,
    part,
    slots_a,
    slots_b,
    slots_c,
    load_sem,
    out_sem,
    xs_sem,
    xr_sem,
    ys_sem,
    yr_sem,
    zs_sem,
    zr_sem,
    ts_sem,
    tr_sem,
):
    px, py, pz = lax.axis_index("gx"), lax.axis_index("gy"), lax.axis_index("gz")
    nx, ny, nz = lax.axis_size("gx"), lax.axis_size("gy"), lax.axis_size("gz")
    core = pz % 2
    zl = (pz // 2) % 2
    field_in = [density, momentum.at[0], momentum.at[1], momentum.at[2], energy]
    field_out = [new_density, new_momentum.at[0], new_momentum.at[1], new_momentum.at[2], new_energy]

    flag_copy = pltpu.make_async_copy(flags, flag, load_sem.at[8])
    flag_copy.start()
    loads = [pltpu.make_async_copy(field_in[f], q.at[f], load_sem.at[f]) for f in range(5)]
    disp_loads = [
        pltpu.make_async_copy(displacement.at[a], disp.at[a], load_sem.at[5 + a]) for a in range(3)
    ]
    loads[0].start()
    loads[4].start()
    for copy in disp_loads:
        copy.start()
    for f in (1, 2, 3):
        loads[f].start()

    def place(x=None, y=None, z=None):
        target = {}
        if x is not None:
            target["gx"] = x
        if y is not None:
            target["gy"] = y
        if z is not None:
            target["gz"] = z
        return target

    def along_z(step):
        chip = lax.rem(py * 2 + zl + step, 2 * ny)
        return place(y=chip // 2, z=pz + 2 * (chip % 2 - zl))

    stage_a = [
        place(x=lax.rem(px + dx, nx), z=pz + dc * (1 - 2 * core))
        for dc in range(2)
        for dx in range(4)
        if dx or dc
    ]
    stage_b = [place(z=lax.rem(pz + 4 * dy, nz)) for dy in range(1, 4)]
    stage_c = [along_z(step) for step in range(1, 8)]
    across = place(z=lax.rem(pz + nz + 2 * core - 1, nz))
    near = stage_a + stage_b + [along_z(step) for step in (1, 2, 6, 7)] + [across]

    barrier = pltpu.get_barrier_semaphore()
    for peer in near:
        pl.semaphore_signal(barrier, inc=1, device_id=peer, device_id_type=MESH)

    flag_copy.wait()
    loads[0].wait()
    loads[4].wait()
    for copy in disp_loads:
        copy.wait()

    flag_open = [flag[i].astype(jnp.float32) for i in range(6)]
    first = [px == 0, py == 0, pz == 0]
    final = [px == nx - 1, py == ny - 1, pz == nz - 1]
    low_scale = [jnp.where(first[a], flag_open[2 * a], 1.0) for a in range(3)]
    gain = [jnp.where(first[a], flag_open[2 * a] * STEP, 0.0) for a in range(3)]
    loss = [jnp.where(final[a], flag_open[2 * a + 1] * -STEP, 0.0) for a in range(3)]

    rows = lax.broadcasted_iota(jnp.int32, (64, 128), 0)
    lanes = lax.broadcasted_iota(jnp.int32, (64, 128), 1)
    weight_y = jnp.where(rows == 0, gain[1], jnp.where(rows == 63, loss[1], 0.0))
    weight_z = jnp.where(lanes == 0, gain[2], jnp.where(lanes == 127, loss[2], 0.0))

    def fold(block):
        return jnp.sum(block.reshape(8, 8, 128), axis=0)

    def plane_sum(x, sums):
        weight = (
            1.0
            + weight_y * disp[1, x].astype(jnp.float32)
            + weight_z * disp[2, x].astype(jnp.float32)
        )
        return (sums[0] + fold(q[0, x] * weight), sums[1] + fold(q[4, x] * weight))

    weight_low = gain[0] * disp[0, 0].astype(jnp.float32)
    weight_high = loss[0] * disp[0, 7].astype(jnp.float32)
    sums = tuple(fold(q[f, 0] * weight_low + q[f, 7] * weight_high) for f in (0, 4))
    sums = lax.fori_loop(0, 8, plane_sum, sums)
    row8 = lax.broadcasted_iota(jnp.int32, (8, 128), 0)
    part[0] = jnp.where(
        row8 == 0,
        jnp.sum(sums[0], axis=0, keepdims=True),
        jnp.where(row8 == 1, jnp.sum(sums[1], axis=0, keepdims=True), 0.0),
    )
    for f in (1, 2, 3):
        loads[f].wait()

    pl.semaphore_wait(barrier, len(near))

    def total_copies(stage, peers, slots, base):
        return [
            pltpu.make_async_remote_copy(
                src_ref=part.at[stage],
                dst_ref=slots.at[i],
                send_sem=ts_sem.at[base + i],
                recv_sem=tr_sem.at[base + i],
                device_id=peer,
                device_id_type=MESH,
            )
            for i, peer in enumerate(peers)
        ]

    copies_a = total_copies(0, stage_a, slots_a, 0)
    copies_b = total_copies(1, stage_b, slots_b, 7)
    copies_c = total_copies(2, stage_c, slots_c, 10)
    for copy in copies_a:
        copy.start()

    def remote(src, dst, send_sem, recv_sem, peer):
        return pltpu.make_async_remote_copy(
            src_ref=src,
            dst_ref=dst,
            send_sem=send_sem,
            recv_sem=recv_sem,
            device_id=peer,
            device_id_type=MESH,
        )

    x_next = place(x=lax.rem(px + 1, nx))
    x_prev = place(x=lax.rem(px + nx - 1, nx))
    face_copy = remote(disp.at[0, 0], xface, xs_sem.at[10], xr_sem.at[10], x_prev)
    up_copies = [
        remote(q.at[f, pl.ds(6, 2)], xlow.at[f], xs_sem.at[f], xr_sem.at[f], x_next) for f in range(5)
    ]
    down_copies = [
        remote(q.at[f, pl.ds(0, 2)], xhigh.at[f], xs_sem.at[5 + f], xr_sem.at[5 + f], x_prev)
        for f in range(5)
    ]

    @pl.when(jnp.logical_not(first[0]))
    def _():
        face_copy.start()

    for f in range(5):

        @pl.when(jnp.logical_not(final[0]))
        def _():
            up_copies[f].start()

        @pl.when(jnp.logical_not(first[0]))
        def _():
            down_copies[f].start()

    for f in range(5):
        for r in range(2):
            yup[2 * f + r] = q[f, :, 62 + r, :]
            ydown[2 * f + r] = q[f, :, r, :]
    ydown[10] = disp[1, :, 0, :].astype(jnp.float32) * STEP

    y_copies = [
        remote(yup, ylow, ys_sem.at[0], yr_sem.at[0], place(y=lax.rem(py + 1, ny))),
        remote(ydown, yhigh, ys_sem.at[1], yr_sem.at[1], place(y=lax.rem(py + ny - 1, ny))),
    ]
    for copy in y_copies:
        copy.start()

    lane8 = lax.broadcasted_iota(jnp.int32, (8, 128), 1)
    slot_of = lane8 // 4
    place4 = lane8 % 4

    def pack(source, base, half):
        packed = jnp.zeros((8, 128), jnp.float32)
        for xx in range(4):
            plane = source[base, half * 4 + xx].astype(jnp.float32)
            for t in range(8):
                k = xx * 8 + t
                moved = pltpu.roll(plane[8 * t : 8 * t + 8], (4 * k + 2) % 128, 1)
                packed = jnp.where(slot_of == k, moved, packed)
        return packed

    for f in range(5):
        for half in range(2):
            zpack[2 * f + half] = pack(q, f, half)
    for half in range(2):
        zpack[10 + half] = pack(disp, 2, half) * STEP

    z_copies = [
        remote(zpack, zlow, zs_sem.at[0], zr_sem.at[0], place(z=lax.rem(pz + 1, nz))),
        remote(zpack, zhigh, zs_sem.at[1], zr_sem.at[1], place(z=lax.rem(pz + nz - 1, nz))),
    ]
    for copy in z_copies:
        copy.start()

    for copy in copies_a:
        copy.wait_recv()
    part[1] = part[0] + jnp.sum(slots_a[...], axis=0)
    for copy in copies_b:
        copy.start()

    for copy in y_copies:
        copy.wait_recv()
    v0 = disp[1, :, 0, :].astype(jnp.float32) * (STEP * low_scale[1])
    v_last = disp[1, :, 63, :].astype(jnp.float32) * (STEP * flag_open[3])
    v64 = jnp.where(final[1], v_last, yhigh[10])
    g64 = half_weight(v64)
    for f in range(5):
        q0, qa, qb = q[f, :, 0, :], q[f, :, 62, :], q[f, :, 63, :]
        lo1 = jnp.where(first[1], q0, ylow[2 * f + 1])
        lo2 = jnp.where(first[1], q0, ylow[2 * f])
        hi0 = jnp.where(final[1], qb, yhigh[2 * f])
        hi1 = jnp.where(final[1], qb, yhigh[2 * f + 1])
        d64 = hi0 - qb
        s63 = minmod(qb - qa, d64)
        s64 = minmod(d64, hi1 - hi0)
        yedge[0, f] = lo1
        yedge[1, f] = d64
        yedge[2, f] = minmod(lo1 - lo2, q0 - lo1)
        yedge[3, f] = v64 * jnp.where(v64 > 0, qb, hi0) + g64 * jnp.where(v64 > 0, s63, s64)

    for copy in z_copies:
        copy.wait_recv()

    def face(four, v):
        behind = back(four)
        diff = four - behind
        slope = minmod(diff, ahead(diff))
        flux = v * jnp.where(v > 0, behind, four) + half_weight(v) * jnp.where(
            v > 0, back(slope), slope
        )
        return slope, flux

    for half in range(2):
        own_v = zpack[10 + half]
        v_low = own_v * low_scale[2]
        v_high = jnp.where(final[2], back(own_v) * flag_open[5], zhigh[10 + half])
        zface[half] = ahead(v_high)
        for f in range(5):
            j = 2 * f + half
            own = zpack[j]
            ghost_low = jnp.where(place4 == 0, pltpu.roll(own, 126, 1), ahead(own))
            ghost_high = jnp.where(place4 == 2, back(own), pltpu.roll(own, 2, 1))
            low = jnp.where(place4 < 2, jnp.where(first[2], ghost_low, zlow[j]), own)
            high = jnp.where(place4 < 2, own, jnp.where(final[2], ghost_high, zhigh[j]))
            slope_low, flux_low = face(low, v_low)
            slope_high, flux_high = face(high, v_high)
            zslope[j] = jnp.where(place4 == 1, slope_high, slope_low)
            zflow[j] = jnp.where(
                place4 == 1,
                ahead(jnp.where(v_high > 0, 0.0, flux_high)),
                jnp.where(v_low > 0, flux_low, 0.0),
            )

    scale_y = jnp.where(rows == 0, STEP * low_scale[1], STEP)
    scale_z = jnp.where(lanes == 0, STEP * low_scale[2], STEP)

    def planes(x, carry):
        half = x // 4
        moves = [lax.rem(128 + 126 - 4 * ((x % 4) * 8 + t), 128) for t in range(8)]

        def spread(packed):
            return jnp.concatenate([pltpu.roll(packed, move, 1) for move in moves], 0)

        vy = disp[1, x].astype(jnp.float32) * scale_y
        gy = half_weight(vy)
        up_y = vy > 0
        vz = disp[2, x].astype(jnp.float32) * scale_z
        vz_next = jnp.where(lanes == 127, spread(zface[half]), ahead(vz))
        right = jnp.maximum(vz_next, 0.0)
        right_w = 0.5 * right * (1.0 - right)
        left = jnp.minimum(vz, 0.0)
        left_w = -0.5 * left * (1.0 + left)
        at_first, at_last = lanes == 0, lanes == 127
        at_edge = jnp.logical_or(at_first, at_last)
        for f in range(5):
            value = q[f, x]

            below = back(value)
            above = ahead(value)
            slope = minmod(value - below, above - value)
            slope = jnp.where(at_edge, spread(zslope[2 * f + half]), slope)
            flow = spread(zflow[2 * f + half])
            out_right = right * value + right_w * slope
            out_left = left * value + left_w * slope
            from_left = jnp.where(at_first, flow, back(out_right))
            from_right = jnp.where(at_last, flow, ahead(out_left))
            change_z = (from_left - out_right) + (out_left - from_right)

            below = shift_down(value, yedge[0, f, pl.ds(x, 1), :])
            diff = value - below
            slope = minmod(diff, shift_up(diff, yedge[1, f, pl.ds(x, 1), :]))
            slope_below = shift_down(slope, yedge[2, f, pl.ds(x, 1), :])
            flux = vy * jnp.where(up_y, below, value) + gy * jnp.where(up_y, slope_below, slope)
            change_y = flux - shift_up(flux, yedge[3, f, pl.ds(x, 1), :])
            acc[f, x] = (value + change_y) + change_z
        return carry

    lax.fori_loop(0, 4, planes, 0)
    for copy in copies_b:
        copy.wait_recv()
    part[2] = part[1] + jnp.sum(slots_b[...], axis=0)
    for copy in copies_c:
        copy.start()
    lax.fori_loop(4, 8, planes, 0)

    @pl.when(jnp.logical_not(final[0]))
    def _():
        face_copy.wait_recv()

    for i in range(9):
        if i == 0:
            v = disp[0, 0].astype(jnp.float32) * (STEP * low_scale[0])
        elif i < 8:
            v = disp[0, i].astype(jnp.float32) * STEP
        else:
            v_last = disp[0, 7].astype(jnp.float32) * (STEP * flag_open[1])
            v = jnp.where(final[0], v_last, xface[...].astype(jnp.float32) * STEP)
        vx[i] = v
        gx_w[i] = half_weight(v)

    stores = []
    for f in range(5):

        @pl.when(jnp.logical_not(first[0]))
        def _():
            up_copies[f].wait_recv()

        @pl.when(jnp.logical_not(final[0]))
        def _():
            down_copies[f].wait_recv()

        def tile(t, carry):
            part_rows = pl.ds(pl.multiple_of(t * 8, 8), 8)
            own = [q[f, i, part_rows] for i in range(8)]
            cell = (
                [jnp.where(first[0], own[0], xlow[f, r, part_rows]) for r in range(2)]
                + own
                + [jnp.where(final[0], own[7], xhigh[f, r, part_rows]) for r in range(2)]
            )
            diff = [cell[i + 1] - cell[i] for i in range(11)]
            slope = [minmod(diff[i], diff[i + 1]) for i in range(10)]
            flux = []
            for i in range(9):
                v = vx[i, part_rows]
                g = gx_w[i, part_rows]
                flux.append(
                    v * jnp.where(v > 0, cell[i + 1], cell[i + 2])
                    + g * jnp.where(v > 0, slope[i], slope[i + 1])
                )
            for i in range(8):
                acc[f, i, part_rows] += flux[i] - flux[i + 1]
            return carry

        lax.fori_loop(0, 8, tile, 0)
        store = pltpu.make_async_copy(acc.at[f], field_out[f], out_sem.at[f])
        store.start()
        stores.append(store)

    for copy in copies_c:
        copy.wait_recv()
    grand = part[2] + jnp.sum(slots_c[...], axis=0)
    totals[0] = jnp.sum(grand[0:1]) / cells
    totals[1] = jnp.sum(grand[1:2]) / cells

    for copy in copies_a + copies_b + copies_c + y_copies + z_copies:
        copy.wait_send()

    @pl.when(jnp.logical_not(first[0]))
    def _():
        face_copy.wait_send()

    for f in range(5):

        @pl.when(jnp.logical_not(final[0]))
        def _():
            up_copies[f].wait_send()

        @pl.when(jnp.logical_not(first[0]))
        def _():
            down_copies[f].wait_send()

    for store in stores:
        store.wait()


def shards(cells, density, momentum, energy, displacement, flags):
    f32, i32 = jnp.float32, jnp.int32
    anywhere = pl.BlockSpec(memory_space=pl.ANY)
    return pl.pallas_call(
        functools.partial(kernel, cells),
        out_shape=(
            jax.ShapeDtypeStruct(density.shape, f32),
            jax.ShapeDtypeStruct(momentum.shape, f32),
            jax.ShapeDtypeStruct(energy.shape, f32),
            jax.ShapeDtypeStruct((2,), f32),
        ),
        in_specs=[anywhere] * 5,
        out_specs=(anywhere, anywhere, anywhere, pl.BlockSpec(memory_space=pltpu.SMEM)),
        scratch_shapes=[
            pltpu.VMEM((5, 8, 64, 128), f32),
            pltpu.VMEM((3, 8, 64, 128), i32),
            pltpu.SMEM((6,), i32),
            pltpu.VMEM((5, 8, 64, 128), f32),
            pltpu.VMEM((9, 64, 128), f32),
            pltpu.VMEM((9, 64, 128), f32),
            pltpu.VMEM((5, 2, 64, 128), f32),
            pltpu.VMEM((5, 2, 64, 128), f32),
            pltpu.VMEM((64, 128), i32),
            pltpu.VMEM((10, 8, 128), f32),
            pltpu.VMEM((11, 8, 128), f32),
            pltpu.VMEM((10, 8, 128), f32),
            pltpu.VMEM((11, 8, 128), f32),
            pltpu.VMEM((4, 5, 8, 128), f32),
            pltpu.VMEM((12, 8, 128), f32),
            pltpu.VMEM((12, 8, 128), f32),
            pltpu.VMEM((12, 8, 128), f32),
            pltpu.VMEM((10, 8, 128), f32),
            pltpu.VMEM((10, 8, 128), f32),
            pltpu.VMEM((2, 8, 128), f32),
            pltpu.VMEM((3, 8, 128), f32),
            pltpu.VMEM((7, 8, 128), f32),
            pltpu.VMEM((3, 8, 128), f32),
            pltpu.VMEM((7, 8, 128), f32),
            pltpu.SemaphoreType.DMA((9,)),
            pltpu.SemaphoreType.DMA((5,)),
            pltpu.SemaphoreType.DMA((11,)),
            pltpu.SemaphoreType.DMA((11,)),
            pltpu.SemaphoreType.DMA((2,)),
            pltpu.SemaphoreType.DMA((2,)),
            pltpu.SemaphoreType.DMA((2,)),
            pltpu.SemaphoreType.DMA((2,)),
            pltpu.SemaphoreType.DMA((17,)),
            pltpu.SemaphoreType.DMA((17,)),
        ],
        compiler_params=pltpu.CompilerParams(collective_id=0, has_side_effects=True),
        name="remap",
    )(density, momentum, energy, displacement, flags)


def solution(mesh):
    cells = float(mesh.shape["gx"] * mesh.shape["gy"] * mesh.shape["gz"] * 8 * 64 * 128)
    block = P("gx", "gy", "gz")
    three = P(None, "gx", "gy", "gz")
    return jax.shard_map(
        functools.partial(shards, cells),
        mesh=mesh,
        in_specs=(block, three, block, three, P()),
        out_specs=(block, three, block, P()),
        check_vma=False,
    )
```

time: 132 us -> 28 us (0.21)
  the two profiles are of different devices: /device:TPU:5 before, /device:TPU:1 now
where the time goes in v1:
time: 28 us; the launch traced here: 27.5 us
  Pallas kernels  21.8 us (78%)
  local copies, waits for them, and re-layouts  5.02 us (18%)
  between operations  0.64 us (2%)
    pallas_call x1, Pallas kernels, shards(): pl.pallas_call(functools.partial(kernel, cells), out_shape=(jax.ShapeDtyp...  21.8 us
    unnamed x8, local copies, waits for them, and re-layouts  5.02 us

profile of v1, /device:TPU:1, one launch (start us, length us, event | category | flops | bytes accessed | tf_op | source)
XLA Modules:
  0.0 27.5 jit_solution(504093219221708076)
XLA Ops:
  0.6 21.8 %remap.1 = (f32[8,64,128]{2,1,0:T(8,128)}, f32[3,8,64,128]{3,2,1,0:T(8,128)}, f32[8,64,128]{2,1,0:T(8,128)}, f32[2]{0:T(128)}) custom-call(f32[8,64,128]{2,1,0:T(8,128)} %density.1, f32[3,8,64,128]{3,2,1,0:T(8,128)} %momentum.1, f32[8,64,128]{2,1,0:T(8,128)} %energy.1, s32[3,8,64,128]{3,2,1,0:T(8,128)} %displacement.1, s32[6]{0:T(128)} %flags.1), custom_call_target="tpu_custom_call" | custom-call | tf_op jit(solution)/shard_map/remap/pallas_call | solution.py:475
  22.5 1.7 %copy.13 = f32[8,64,128]{2,1,0:T(8,128)} copy(f32[8,64,128]{2,1,0:T(8,128)} %get-tuple-element.8) | data formatting | bytes 524288
  24.2 0.0 copy-start
  24.2 2.1 %copy.14 = f32[3,8,64,128]{3,2,1,0:T(8,128)} copy(f32[3,8,64,128]{3,2,1,0:T(8,128)} %get-tuple-element.9) | data formatting | bytes 1572864
  26.3 0.0 copy-done
  26.3 0.0 copy-start.1
  26.3 0.7 %copy.15 = f32[8,64,128]{2,1,0:T(8,128)} copy(f32[8,64,128]{2,1,0:T(8,128)S(1)} %copy-done) | data formatting | bytes 524288
  27.0 0.0 copy-done.1
  27.0 0.5 %copy.16 = f32[2]{0:T(128)} copy(f32[2]{0:T(128)S(1)} %copy-done.1) | data formatting | bytes 16
Async XLA Ops:
  24.2 2.1 %copy-start = (f32[8,64,128]{2,1,0:T(8,128)S(1)}, f32[8,64,128]{2,1,0:T(8,128)}, u32[]{:S(2)}) copy-start(f32[8,64,128]{2,1,0:T(8,128)} %get-tuple-element.10) | copy-start | bytes 786436
  26.3 0.7 %copy-start.1 = (f32[2]{0:T(128)S(1)}, f32[2]{0:T(128)}, u32[]{:S(2)}) copy-start(f32[2]{0:T(128)} %get-tuple-element.11) | copy-start | bytes 28

commit v2 on v1

--- a/solution.py
+++ b/solution.py
@@ -46,20 +46,16 @@
 
 
 def kernel(
-    cells,
     density,
     momentum,
     energy,
     displacement,
     flags,
-    new_density,
-    new_momentum,
-    new_energy,
-    totals,
+    acc,
+    grand,
     q,
     disp,
     flag,
-    acc,
     vx,
     gx_w,
     xlow,
@@ -79,9 +75,7 @@
     part,
     slots_a,
     slots_b,
-    slots_c,
     load_sem,
-    out_sem,
     xs_sem,
     xr_sem,
     ys_sem,
@@ -90,13 +84,13 @@
     zr_sem,
     ts_sem,
     tr_sem,
+    round_sem,
 ):
     px, py, pz = lax.axis_index("gx"), lax.axis_index("gy"), lax.axis_index("gz")
     nx, ny, nz = lax.axis_size("gx"), lax.axis_size("gy"), lax.axis_size("gz")
     core = pz % 2
     zl = (pz // 2) % 2
     field_in = [density, momentum.at[0], momentum.at[1], momentum.at[2], energy]
-    field_out = [new_density, new_momentum.at[0], new_momentum.at[1], new_momentum.at[2], new_energy]
 
     flag_copy = pltpu.make_async_copy(flags, flag, load_sem.at[8])
     flag_copy.start()
@@ -121,9 +115,9 @@
             target["gz"] = z
         return target
 
-    def along_z(step):
-        chip = lax.rem(py * 2 + zl + step, 2 * ny)
-        return place(y=chip // 2, z=pz + 2 * (chip % 2 - zl))
+    def along_yz(dy, dz):
+        chip = lax.rem(py * 2 + zl + dz, 2 * ny)
+        return place(y=chip // 2, z=lax.rem(pz + 4 * dy, nz) + 2 * (chip % 2 - zl))
 
     stage_a = [
         place(x=lax.rem(px + dx, nx), z=pz + dc * (1 - 2 * core))
@@ -131,10 +125,10 @@
         for dx in range(4)
         if dx or dc
     ]
-    stage_b = [place(z=lax.rem(pz + 4 * dy, nz)) for dy in range(1, 4)]
-    stage_c = [along_z(step) for step in range(1, 8)]
+    stage_b = [along_yz(dy, dz) for dy in range(4) for dz in range(8) if dy or dz]
+    beside = [along_yz(0, dz) for dz in (1, 2, 6, 7)] + [along_yz(dy, 0) for dy in (1, 2, 3)]
     across = place(z=lax.rem(pz + nz + 2 * core - 1, nz))
-    near = stage_a + stage_b + [along_z(step) for step in (1, 2, 6, 7)] + [across]
+    near = stage_a + beside + [across]
 
     barrier = pltpu.get_barrier_semaphore()
     for peer in near:
@@ -173,12 +167,14 @@
     weight_high = loss[0] * disp[0, 7].astype(jnp.float32)
     sums = tuple(fold(q[f, 0] * weight_low + q[f, 7] * weight_high) for f in (0, 4))
     sums = lax.fori_loop(0, 8, plane_sum, sums)
-    row8 = lax.broadcasted_iota(jnp.int32, (8, 128), 0)
-    part[0] = jnp.where(
-        row8 == 0,
-        jnp.sum(sums[0], axis=0, keepdims=True),
-        jnp.where(row8 == 1, jnp.sum(sums[1], axis=0, keepdims=True), 0.0),
-    )
+    lane1 = lax.broadcasted_iota(jnp.int32, (1, 128), 1)
+
+    def halves(low, high):
+        low = jnp.sum(low, axis=0, keepdims=True)
+        high = jnp.sum(high, axis=0, keepdims=True)
+        return jnp.where(lane1 < 64, low + pltpu.roll(low, 64, 1), high + pltpu.roll(high, 64, 1))
+
+    part[0] = halves(*sums)
     for f in (1, 2, 3):
         loads[f].wait()
 
@@ -199,9 +195,10 @@
 
     copies_a = total_copies(0, stage_a, slots_a, 0)
     copies_b = total_copies(1, stage_b, slots_b, 7)
-    copies_c = total_copies(2, stage_c, slots_c, 10)
     for copy in copies_a:
         copy.start()
+    for peer in beside:
+        pl.semaphore_signal(round_sem.at[0], inc=1, device_id=peer, device_id_type=MESH)
 
     def remote(src, dst, send_sem, recv_sem, peer):
         return pltpu.make_async_remote_copy(
@@ -278,9 +275,13 @@
     for copy in z_copies:
         copy.start()
 
+    pl.semaphore_wait(round_sem.at[0], len(beside))
+    for peer in beside:
+        pl.semaphore_signal(round_sem.at[1], inc=1, device_id=peer, device_id_type=MESH)
     for copy in copies_a:
         copy.wait_recv()
     part[1] = part[0] + jnp.sum(slots_a[...], axis=0)
+    pl.semaphore_wait(round_sem.at[1], len(beside))
     for copy in copies_b:
         copy.start()
 
@@ -381,13 +382,7 @@
             acc[f, x] = (value + change_y) + change_z
         return carry
 
-    lax.fori_loop(0, 4, planes, 0)
-    for copy in copies_b:
-        copy.wait_recv()
-    part[2] = part[1] + jnp.sum(slots_b[...], axis=0)
-    for copy in copies_c:
-        copy.start()
-    lax.fori_loop(4, 8, planes, 0)
+    lax.fori_loop(0, 8, planes, 0)
 
     @pl.when(jnp.logical_not(final[0]))
     def _():
@@ -404,7 +399,6 @@
         vx[i] = v
         gx_w[i] = half_weight(v)
 
-    stores = []
     for f in range(5):
 
         @pl.when(jnp.logical_not(first[0]))
@@ -438,17 +432,12 @@
             return carry
 
         lax.fori_loop(0, 8, tile, 0)
-        store = pltpu.make_async_copy(acc.at[f], field_out[f], out_sem.at[f])
-        store.start()
-        stores.append(store)
-
-    for copy in copies_c:
+
+    for copy in copies_b:
         copy.wait_recv()
-    grand = part[2] + jnp.sum(slots_c[...], axis=0)
-    totals[0] = jnp.sum(grand[0:1]) / cells
-    totals[1] = jnp.sum(grand[1:2]) / cells
-
-    for copy in copies_a + copies_b + copies_c + y_copies + z_copies:
+    grand[...] = part[1] + jnp.sum(slots_b[...], axis=0)
+
+    for copy in copies_a + copies_b + y_copies + z_copies:
         copy.wait_send()
 
     @pl.when(jnp.logical_not(first[0]))
@@ -465,28 +454,46 @@
         def _():
             down_copies[f].wait_send()
 
+
+def write_out(cells, acc, grand, new_density, new_momentum, new_energy, totals, pair, sem):
+    stores = [
+        pltpu.make_async_copy(acc.at[0], new_density, sem.at[0]),
+        pltpu.make_async_copy(acc.at[pl.ds(1, 3)], new_momentum, sem.at[1]),
+        pltpu.make_async_copy(acc.at[4], new_energy, sem.at[2]),
+    ]
+    for store in stores:
+        store.start()
+    lane1 = lax.broadcasted_iota(jnp.int32, (1, 128), 1)
+    both = grand[...]
+    pair[0] = jnp.sum(jnp.where(lane1 < 64, both, 0.0)) / cells
+    pair[1] = jnp.sum(jnp.where(lane1 < 64, 0.0, both)) / cells
+    last = pltpu.make_async_copy(pair, totals, sem.at[3])
+    last.start()
     for store in stores:
         store.wait()
+    last.wait()
 
 
 def shards(cells, density, momentum, energy, displacement, flags):
     f32, i32 = jnp.float32, jnp.int32
-    anywhere = pl.BlockSpec(memory_space=pl.ANY)
-    return pl.pallas_call(
-        functools.partial(kernel, cells),
+    anywhere = pl.BlockSpec(memory_space=pltpu.HBM)
+    local = pl.BlockSpec(memory_space=pltpu.VMEM)
+    inputs = [
+        pltpu.with_memory_space_constraint(a, pltpu.HBM)
+        for a in (density, momentum, energy, displacement, flags)
+    ]
+    acc, grand = pl.pallas_call(
+        kernel,
         out_shape=(
-            jax.ShapeDtypeStruct(density.shape, f32),
-            jax.ShapeDtypeStruct(momentum.shape, f32),
-            jax.ShapeDtypeStruct(energy.shape, f32),
-            jax.ShapeDtypeStruct((2,), f32),
+            jax.ShapeDtypeStruct((5, 8, 64, 128), f32),
+            jax.ShapeDtypeStruct((1, 128), f32),
         ),
         in_specs=[anywhere] * 5,
-        out_specs=(anywhere, anywhere, anywhere, pl.BlockSpec(memory_space=pltpu.SMEM)),
+        out_specs=(local, local),
         scratch_shapes=[
             pltpu.VMEM((5, 8, 64, 128), f32),
             pltpu.VMEM((3, 8, 64, 128), i32),
             pltpu.SMEM((6,), i32),
-            pltpu.VMEM((5, 8, 64, 128), f32),
             pltpu.VMEM((9, 64, 128), f32),
             pltpu.VMEM((9, 64, 128), f32),
             pltpu.VMEM((5, 2, 64, 128), f32),
@@ -503,24 +510,39 @@
             pltpu.VMEM((10, 8, 128), f32),
             pltpu.VMEM((10, 8, 128), f32),
             pltpu.VMEM((2, 8, 128), f32),
-            pltpu.VMEM((3, 8, 128), f32),
-            pltpu.VMEM((7, 8, 128), f32),
-            pltpu.VMEM((3, 8, 128), f32),
-            pltpu.VMEM((7, 8, 128), f32),
+            pltpu.VMEM((2, 1, 128), f32),
+            pltpu.VMEM((7, 1, 128), f32),
+            pltpu.VMEM((31, 1, 128), f32),
             pltpu.SemaphoreType.DMA((9,)),
-            pltpu.SemaphoreType.DMA((5,)),
             pltpu.SemaphoreType.DMA((11,)),
             pltpu.SemaphoreType.DMA((11,)),
             pltpu.SemaphoreType.DMA((2,)),
             pltpu.SemaphoreType.DMA((2,)),
             pltpu.SemaphoreType.DMA((2,)),
             pltpu.SemaphoreType.DMA((2,)),
-            pltpu.SemaphoreType.DMA((17,)),
-            pltpu.SemaphoreType.DMA((17,)),
+            pltpu.SemaphoreType.DMA((38,)),
+            pltpu.SemaphoreType.DMA((38,)),
+            pltpu.SemaphoreType.REGULAR((2,)),
         ],
-        compiler_params=pltpu.CompilerParams(collective_id=0, has_side_effects=True),
+        compiler_params=pltpu.CompilerParams(
+            collective_id=0, has_side_effects=True, vmem_limit_bytes=16 * 2**20
+        ),
         name="remap",
-    )(density, momentum, energy, displacement, flags)
+    )(*inputs)
+    return pl.pallas_call(
+        functools.partial(write_out, cells),
+        out_shape=(
+            jax.ShapeDtypeStruct(density.shape, f32),
+            jax.ShapeDtypeStruct(momentum.shape, f32),
+            jax.ShapeDtypeStruct(energy.shape, f32),
+            jax.ShapeDtypeStruct((2,), f32),
+        ),
+        in_specs=[local, local],
+        out_specs=[anywhere] * 4,
+        scratch_shapes=[pltpu.SMEM((2,), f32), pltpu.SemaphoreType.DMA((4,))],
+        compiler_params=pltpu.CompilerParams(vmem_limit_bytes=4 * 2**20),
+        name="write_out",
+    )(acc, grand)
 
 
 def solution(mesh):

time: 28 us -> 22.4 us (0.80); the launches traced: 27.5 us -> 22.3 us
  local copies, waits for them, and re-layouts: 5.02 us -> 0 us
    unnamed x8 -> x0, local copies, waits for them, and re-layouts: 5.02 us -> none
    pallas_call x1 -> x2, Pallas kernels: 21.8 us -> 21.6 us  [the longest x1 20.5 us: shards(): pl.pallas_call(kernel, out_shape=(jax.ShapeDtypeStruct((5, 8, 64, 128), f...]
where the time goes in v2:
time: 22.4 us; the launch traced here: 22.3 us
  Pallas kernels  21.6 us (96%)
  between operations  0.64 us (3%)
    pallas_call x1, Pallas kernels, shards(): pl.pallas_call(kernel, out_shape=(jax.ShapeDtypeStruct((5, 8, 64, 128), f...  20.5 us
    pallas_call x1, Pallas kernels, shards(): pl.pallas_call(functools.partial(write_out, cells), out_shape=(jax.ShapeD...  1.09 us

profile of v2, /device:TPU:1, one launch (start us, length us, event | category | flops | bytes accessed | tf_op | source)
XLA Modules:
  0.0 22.3 jit_solution(16809849491485921898)
XLA Ops:
  0.6 20.5 %remap.1 = (f32[5,8,64,128]{3,2,1,0:T(8,128)S(1)}, f32[1,128]{1,0:T(1,128)S(1)}) custom-call(f32[8,64,128]{2,1,0:T(8,128)} %density.1, f32[3,8,64,128]{3,2,1,0:T(8,128)} %momentum.1, f32[8,64,128]{2,1,0:T(8,128)} %energy.1, s32[3,8,64,128]{3,2,1,0:T(8,128)} %displacement.1, s32[6]{0:T(128)} %flags.1), custom_call_target="tpu_custom_call" | custom-call | tf_op jit(solution)/shard_map/remap/pallas_call | solution.py:485
  21.2 1.1 %write_out.1 = (f32[8,64,128]{2,1,0:T(8,128)}, f32[3,8,64,128]{3,2,1,0:T(8,128)}, f32[8,64,128]{2,1,0:T(8,128)}, f32[2]{0:T(128)}) custom-call(f32[5,8,64,128]{3,2,1,0:T(8,128)S(1)} %get-tuple-element.6.acc, f32[1,128]{1,0:T(1,128)S(1)} %get-tuple-element.7.grand), custom_call_target="tpu_custom_call" | custom-call | tf_op jit(solution)/shard_map/write_out/pallas_call | solution.py:532

commit v3 on v2

--- a/solution.py
+++ b/solution.py
@@ -9,6 +9,7 @@
 
 MESH = pl.DeviceIdType.MESH
 STEP = 1.0 / 256.0
+EARLY = 3
 
 
 def minmod(left_diff, right_diff):
@@ -20,21 +21,6 @@
 def half_weight(v):
     size = jnp.abs(v)
     return 0.5 * size * (1.0 - size)
-
-
-def shift_down(block, first_row):
-    moved = pltpu.roll(block, 1, 0)
-    row = lax.broadcasted_iota(jnp.int32, (8, 128), 0)
-    top = jnp.where(row == 0, first_row, moved[:8])
-    return jnp.concatenate([top, moved[8:]], 0)
-
-
-def shift_up(block, last_row):
-    n = block.shape[0]
-    moved = pltpu.roll(block, n - 1, 0)
-    row = lax.broadcasted_iota(jnp.int32, (8, 128), 0)
-    bottom = jnp.where(row == 7, last_row, moved[n - 8 :])
-    return jnp.concatenate([moved[: n - 8], bottom], 0)
 
 
 def back(block):
@@ -65,13 +51,10 @@
     ydown,
     ylow,
     yhigh,
-    yedge,
     zpack,
     zlow,
     zhigh,
-    zslope,
-    zflow,
-    zface,
+    zcorr,
     part,
     slots_a,
     slots_b,
@@ -85,6 +68,7 @@
     ts_sem,
     tr_sem,
     round_sem,
+    reply_sem,
 ):
     px, py, pz = lax.axis_index("gx"), lax.axis_index("gy"), lax.axis_index("gz")
     nx, ny, nz = lax.axis_size("gx"), lax.axis_size("gy"), lax.axis_size("gz")
@@ -115,9 +99,16 @@
             target["gz"] = z
         return target
 
+    level = py * 2 + zl
+    levels = 2 * ny
+    early = level < EARLY
+
     def along_yz(dy, dz):
-        chip = lax.rem(py * 2 + zl + dz, 2 * ny)
+        chip = lax.rem(level + dz, levels)
         return place(y=chip // 2, z=lax.rem(pz + 4 * dy, nz) + 2 * (chip % 2 - zl))
+
+    def greet(sem, peer):
+        pl.semaphore_signal(sem, inc=1, device_id=peer, device_id_type=MESH)
 
     stage_a = [
         place(x=lax.rem(px + dx, nx), z=pz + dc * (1 - 2 * core))
@@ -126,13 +117,42 @@
         if dx or dc
     ]
     stage_b = [along_yz(dy, dz) for dy in range(4) for dz in range(8) if dy or dz]
-    beside = [along_yz(0, dz) for dz in (1, 2, 6, 7)] + [along_yz(dy, 0) for dy in (1, 2, 3)]
+    along_y = [along_yz(dy, 0) for dy in (1, 2, 3)]
+    steps = [-2, -1, 1, 2]
+    late_step = [
+        jnp.logical_and(level + step >= EARLY, level + step < levels) for step in steps
+    ]
+    late_steps = sum(ok.astype(jnp.int32) for ok in late_step)
+    has_across = jnp.where(core == 1, pz < nz - 1, pz > 0)
     across = place(z=lax.rem(pz + nz + 2 * core - 1, nz))
-    near = stage_a + beside + [across]
+
+    def greet_late(sem):
+        for step, ok in zip(steps, late_step):
+
+            @pl.when(ok)
+            def _():
+                greet(sem, along_yz(0, step % 8))
 
     barrier = pltpu.get_barrier_semaphore()
-    for peer in near:
-        pl.semaphore_signal(barrier, inc=1, device_id=peer, device_id_type=MESH)
+    for peer in stage_a + along_y:
+        greet(barrier, peer)
+
+    @pl.when(has_across)
+    def _():
+        greet(barrier, across)
+
+    @pl.when(early)
+    def _():
+        for dz in range(1, 8):
+
+            @pl.when(level + dz < levels)
+            def _():
+                for dy in range(4):
+                    greet(barrier, along_yz(dy, dz))
+
+    @pl.when(jnp.logical_not(early))
+    def _():
+        greet_late(barrier)
 
     flag_copy.wait()
     loads[0].wait()
@@ -178,7 +198,13 @@
     for f in (1, 2, 3):
         loads[f].wait()
 
-    pl.semaphore_wait(barrier, len(near))
+    greeted = (
+        len(stage_a)
+        + len(along_y)
+        + has_across.astype(jnp.int32)
+        + jnp.where(early, 4 * level, 4 * EARLY + late_steps)
+    )
+    pl.semaphore_wait(barrier, greeted)
 
     def total_copies(stage, peers, slots, base):
         return [
@@ -197,8 +223,6 @@
     copies_b = total_copies(1, stage_b, slots_b, 7)
     for copy in copies_a:
         copy.start()
-    for peer in beside:
-        pl.semaphore_signal(round_sem.at[0], inc=1, device_id=peer, device_id_type=MESH)
 
     def remote(src, dst, send_sem, recv_sem, peer):
         return pltpu.make_async_remote_copy(
@@ -241,12 +265,32 @@
             ydown[2 * f + r] = q[f, :, r, :]
     ydown[10] = disp[1, :, 0, :].astype(jnp.float32) * STEP
 
-    y_copies = [
-        remote(yup, ylow, ys_sem.at[0], yr_sem.at[0], place(y=lax.rem(py + 1, ny))),
-        remote(ydown, yhigh, ys_sem.at[1], yr_sem.at[1], place(y=lax.rem(py + ny - 1, ny))),
-    ]
-    for copy in y_copies:
-        copy.start()
+    y_up = remote(yup, ylow, ys_sem.at[0], yr_sem.at[0], place(y=lax.rem(py + 1, ny)))
+    y_down = remote(ydown, yhigh, ys_sem.at[1], yr_sem.at[1], place(y=lax.rem(py + ny - 1, ny)))
+
+    for back_step in (1, 2):
+
+        @pl.when(jnp.logical_and(level - back_step >= 0, level - back_step < EARLY))
+        def _():
+            greet(reply_sem.at[0], along_yz(0, 8 - back_step))
+
+    @pl.when(jnp.logical_not(early))
+    def _():
+        greet_late(round_sem.at[0])
+        for peer in along_y:
+            greet(round_sem.at[0], peer)
+
+    @pl.when(jnp.logical_not(first[1]))
+    def _():
+        y_down.start()
+
+    @pl.when(early)
+    def _():
+        pl.semaphore_wait(reply_sem.at[0], 2)
+
+    @pl.when(jnp.logical_not(final[1]))
+    def _():
+        y_up.start()
 
     lane8 = lax.broadcasted_iota(jnp.int32, (8, 128), 1)
     slot_of = lane8 // 4
@@ -268,45 +312,122 @@
     for half in range(2):
         zpack[10 + half] = pack(disp, 2, half) * STEP
 
-    z_copies = [
-        remote(zpack, zlow, zs_sem.at[0], zr_sem.at[0], place(z=lax.rem(pz + 1, nz))),
-        remote(zpack, zhigh, zs_sem.at[1], zr_sem.at[1], place(z=lax.rem(pz + nz - 1, nz))),
-    ]
-    for copy in z_copies:
-        copy.start()
-
-    pl.semaphore_wait(round_sem.at[0], len(beside))
-    for peer in beside:
-        pl.semaphore_signal(round_sem.at[1], inc=1, device_id=peer, device_id_type=MESH)
+    z_up = remote(zpack, zlow, zs_sem.at[0], zr_sem.at[0], place(z=lax.rem(pz + 1, nz)))
+    z_down = remote(zpack, zhigh, zs_sem.at[1], zr_sem.at[1], place(z=lax.rem(pz + nz - 1, nz)))
+
+    @pl.when(jnp.logical_not(final[2]))
+    def _():
+        z_up.start()
+
+    @pl.when(jnp.logical_not(first[2]))
+    def _():
+        z_down.start()
+
+    for target in range(EARLY):
+
+        @pl.when(target < level)
+        def _():
+            for dy in range(4):
+                greet(reply_sem.at[1], along_yz(dy, lax.rem(levels + target - level, levels)))
+
+    scale_y = jnp.where(
+        jnp.logical_or(rows < 2, rows == 63), 0.0, STEP
+    )
+    scale_z = jnp.where(lanes == 0, STEP * low_scale[2], STEP)
+
+    def planes(x, carry):
+        vy = disp[1, x].astype(jnp.float32) * scale_y
+        gy = half_weight(vy)
+        up_y = vy > 0
+        vz = disp[2, x].astype(jnp.float32) * scale_z
+        right = jnp.where(lanes == 127, 0.0, jnp.maximum(ahead(vz), 0.0))
+        right_w = jnp.where(lanes == 0, 0.0, 0.5 * right * (1.0 - right))
+        left = jnp.minimum(vz, 0.0)
+        left_w = jnp.where(
+            jnp.logical_or(lanes == 0, lanes == 127), 0.0, -0.5 * left * (1.0 + left)
+        )
+        for f in range(5):
+            value = q[f, x]
+            below = back(value)
+            above = ahead(value)
+            slope = minmod(value - below, above - value)
+            out_right = right * value + right_w * slope
+            out_left = left * value + left_w * slope
+            change_z = (back(out_right) - out_right) + (out_left - ahead(out_left))
+
+            below = pltpu.roll(value, 1, 0)
+            diff = value - below
+            slope = minmod(diff, pltpu.roll(diff, 63, 0))
+            flux = vy * jnp.where(up_y, below, value) + gy * jnp.where(
+                up_y, pltpu.roll(slope, 1, 0), slope
+            )
+            acc[f, x] = (value + (flux - pltpu.roll(flux, 63, 0))) + change_z
+        return carry
+
+    lax.fori_loop(0, 2, planes, 0)
+
+    @pl.when(jnp.logical_not(early))
+    def _():
+        pl.semaphore_wait(round_sem.at[0], len(along_y) + late_steps)
+        greet_late(round_sem.at[1])
+        for peer in along_y:
+            greet(round_sem.at[1], peer)
+
+    lax.fori_loop(2, 4, planes, 0)
+
     for copy in copies_a:
         copy.wait_recv()
     part[1] = part[0] + jnp.sum(slots_a[...], axis=0)
-    pl.semaphore_wait(round_sem.at[1], len(beside))
-    for copy in copies_b:
-        copy.start()
-
-    for copy in y_copies:
-        copy.wait_recv()
-    v0 = disp[1, :, 0, :].astype(jnp.float32) * (STEP * low_scale[1])
-    v_last = disp[1, :, 63, :].astype(jnp.float32) * (STEP * flag_open[3])
-    v64 = jnp.where(final[1], v_last, yhigh[10])
-    g64 = half_weight(v64)
+
+    @pl.when(jnp.logical_not(early))
+    def _():
+        pl.semaphore_wait(round_sem.at[1], len(along_y) + late_steps)
+        for copy in copies_b:
+            copy.start()
+
+    lax.fori_loop(4, 8, planes, 0)
+
+    @pl.when(jnp.logical_not(first[1]))
+    def _():
+        y_up.wait_recv()
+
+    @pl.when(jnp.logical_not(final[1]))
+    def _():
+        y_down.wait_recv()
+
+    v0, v1, v63 = [disp[1, :, r, :].astype(jnp.float32) * STEP for r in (0, 1, 63)]
+    v64 = jnp.where(final[1], v63 * flag_open[3], yhigh[10])
+    v0 = v0 * low_scale[1]
+
+    def flux_row(v, behind, at, slope_behind, slope_at):
+        return v * jnp.where(v > 0, behind, at) + half_weight(v) * jnp.where(
+            v > 0, slope_behind, slope_at
+        )
+
     for f in range(5):
-        q0, qa, qb = q[f, :, 0, :], q[f, :, 62, :], q[f, :, 63, :]
+        q0, q1, q2, q61, q62, q63 = [q[f, :, r, :] for r in (0, 1, 2, 61, 62, 63)]
         lo1 = jnp.where(first[1], q0, ylow[2 * f + 1])
         lo2 = jnp.where(first[1], q0, ylow[2 * f])
-        hi0 = jnp.where(final[1], qb, yhigh[2 * f])
-        hi1 = jnp.where(final[1], qb, yhigh[2 * f + 1])
-        d64 = hi0 - qb
-        s63 = minmod(qb - qa, d64)
-        s64 = minmod(d64, hi1 - hi0)
-        yedge[0, f] = lo1
-        yedge[1, f] = d64
-        yedge[2, f] = minmod(lo1 - lo2, q0 - lo1)
-        yedge[3, f] = v64 * jnp.where(v64 > 0, qb, hi0) + g64 * jnp.where(v64 > 0, s63, s64)
-
-    for copy in z_copies:
-        copy.wait_recv()
+        hi0 = jnp.where(final[1], q63, yhigh[2 * f])
+        hi1 = jnp.where(final[1], q63, yhigh[2 * f + 1])
+        s0 = minmod(q0 - lo1, q1 - q0)
+        s63 = minmod(q63 - q62, hi0 - q63)
+        flux_0 = flux_row(v0, lo1, q0, minmod(lo1 - lo2, q0 - lo1), s0)
+        flux_1 = flux_row(v1, q0, q1, s0, minmod(q1 - q0, q2 - q1))
+        flux_63 = flux_row(v63, q62, q63, minmod(q62 - q61, q63 - q62), s63)
+        flux_64 = flux_row(v64, q63, hi0, s63, minmod(hi0 - q63, hi1 - hi0))
+        acc[f, :, 0, :] += flux_0 - flux_1
+        acc[f, :, 1, :] += flux_1
+        acc[f, :, 62, :] -= flux_63
+        acc[f, :, 63, :] += flux_63 - flux_64
+
+    @pl.when(jnp.logical_not(first[2]))
+    def _():
+        z_up.wait_recv()
+
+    @pl.when(jnp.logical_not(final[2]))
+    def _():
+        z_down.wait_recv()
 
     def face(four, v):
         behind = back(four)
@@ -319,9 +440,12 @@
 
     for half in range(2):
         own_v = zpack[10 + half]
-        v_low = own_v * low_scale[2]
+        v_low = jnp.where(place4 == 2, own_v * low_scale[2], own_v)
         v_high = jnp.where(final[2], back(own_v) * flag_open[5], zhigh[10 + half])
-        zface[half] = ahead(v_high)
+        left = jnp.minimum(v_low, 0.0)
+        left_w = -0.5 * left * (1.0 + left)
+        right = jnp.maximum(ahead(own_v), 0.0)
+        right_w = 0.5 * right * (1.0 - right)
         for f in range(5):
             j = 2 * f + half
             own = zpack[j]
@@ -331,58 +455,24 @@
             high = jnp.where(place4 < 2, own, jnp.where(final[2], ghost_high, zhigh[j]))
             slope_low, flux_low = face(low, v_low)
             slope_high, flux_high = face(high, v_high)
-            zslope[j] = jnp.where(place4 == 1, slope_high, slope_low)
-            zflow[j] = jnp.where(
-                place4 == 1,
-                ahead(jnp.where(v_high > 0, 0.0, flux_high)),
-                jnp.where(v_low > 0, flux_low, 0.0),
+            by_left = left_w * jnp.where(place4 == 1, slope_high, slope_low)
+            by_right = right_w * slope_low
+            entering = jnp.where(v_low > 0, flux_low, 0.0)
+            zcorr[j] = jnp.where(
+                place4 == 0,
+                -ahead(by_left),
+                jnp.where(
+                    place4 == 1,
+                    by_left - ahead(flux_high) + ahead(left * own),
+                    jnp.where(place4 == 2, entering + by_left - by_right, back(by_right)),
+                ),
             )
 
-    scale_y = jnp.where(rows == 0, STEP * low_scale[1], STEP)
-    scale_z = jnp.where(lanes == 0, STEP * low_scale[2], STEP)
-
-    def planes(x, carry):
-        half = x // 4
-        moves = [lax.rem(128 + 126 - 4 * ((x % 4) * 8 + t), 128) for t in range(8)]
-
-        def spread(packed):
-            return jnp.concatenate([pltpu.roll(packed, move, 1) for move in moves], 0)
-
-        vy = disp[1, x].astype(jnp.float32) * scale_y
-        gy = half_weight(vy)
-        up_y = vy > 0
-        vz = disp[2, x].astype(jnp.float32) * scale_z
-        vz_next = jnp.where(lanes == 127, spread(zface[half]), ahead(vz))
-        right = jnp.maximum(vz_next, 0.0)
-        right_w = 0.5 * right * (1.0 - right)
-        left = jnp.minimum(vz, 0.0)
-        left_w = -0.5 * left * (1.0 + left)
-        at_first, at_last = lanes == 0, lanes == 127
-        at_edge = jnp.logical_or(at_first, at_last)
-        for f in range(5):
-            value = q[f, x]
-
-            below = back(value)
-            above = ahead(value)
-            slope = minmod(value - below, above - value)
-            slope = jnp.where(at_edge, spread(zslope[2 * f + half]), slope)
-            flow = spread(zflow[2 * f + half])
-            out_right = right * value + right_w * slope
-            out_left = left * value + left_w * slope
-            from_left = jnp.where(at_first, flow, back(out_right))
-            from_right = jnp.where(at_last, flow, ahead(out_left))
-            change_z = (from_left - out_right) + (out_left - from_right)
-
-            below = shift_down(value, yedge[0, f, pl.ds(x, 1), :])
-            diff = value - below
-            slope = minmod(diff, shift_up(diff, yedge[1, f, pl.ds(x, 1), :]))
-            slope_below = shift_down(slope, yedge[2, f, pl.ds(x, 1), :])
-            flux = vy * jnp.where(up_y, below, value) + gy * jnp.where(up_y, slope_below, slope)
-            change_y = flux - shift_up(flux, yedge[3, f, pl.ds(x, 1), :])
-            acc[f, x] = (value + change_y) + change_z
-        return carry
-
-    lax.fori_loop(0, 8, planes, 0)
+    @pl.when(early)
+    def _():
+        pl.semaphore_wait(reply_sem.at[1], 4 * (levels - 1 - level))
+        for copy in copies_b:
+            copy.start()
 
     @pl.when(jnp.logical_not(final[0]))
     def _():
@@ -399,6 +489,7 @@
         vx[i] = v
         gx_w[i] = half_weight(v)
 
+    edge_lanes = jnp.logical_or(lane8 < 2, lane8 > 125)
     for f in range(5):
 
         @pl.when(jnp.logical_not(first[0]))
@@ -428,7 +519,10 @@
                     + g * jnp.where(v > 0, slope[i], slope[i + 1])
                 )
             for i in range(8):
-                acc[f, i, part_rows] += flux[i] - flux[i + 1]
+                move = lax.rem(254 - 4 * ((i % 4) * 8 + t), 128)
+                corr = pltpu.roll(zcorr[2 * f + i // 4], move, 1)
+                corr = jnp.where(edge_lanes, corr, 0.0)
+                acc[f, i, part_rows] += (flux[i] - flux[i + 1]) + corr
             return carry
 
         lax.fori_loop(0, 8, tile, 0)
@@ -437,12 +531,23 @@
         copy.wait_recv()
     grand[...] = part[1] + jnp.sum(slots_b[...], axis=0)
 
-    for copy in copies_a + copies_b + y_copies + z_copies:
+    for copy in copies_a + copies_b:
         copy.wait_send()
 
     @pl.when(jnp.logical_not(first[0]))
     def _():
         face_copy.wait_send()
+
+    for copy, there in (
+        (y_up, final[1]),
+        (y_down, first[1]),
+        (z_up, final[2]),
+        (z_down, first[2]),
+    ):
+
+        @pl.when(jnp.logical_not(there))
+        def _():
+            copy.wait_send()
 
     for f in range(5):
 
@@ -503,13 +608,10 @@
             pltpu.VMEM((11, 8, 128), f32),
             pltpu.VMEM((10, 8, 128), f32),
             pltpu.VMEM((11, 8, 128), f32),
-            pltpu.VMEM((4, 5, 8, 128), f32),
             pltpu.VMEM((12, 8, 128), f32),
             pltpu.VMEM((12, 8, 128), f32),
             pltpu.VMEM((12, 8, 128), f32),
             pltpu.VMEM((10, 8, 128), f32),
-            pltpu.VMEM((10, 8, 128), f32),
-            pltpu.VMEM((2, 8, 128), f32),
             pltpu.VMEM((2, 1, 128), f32),
             pltpu.VMEM((7, 1, 128), f32),
             pltpu.VMEM((31, 1, 128), f32),
@@ -522,6 +624,7 @@
             pltpu.SemaphoreType.DMA((2,)),
             pltpu.SemaphoreType.DMA((38,)),
             pltpu.SemaphoreType.DMA((38,)),
+            pltpu.SemaphoreType.REGULAR((2,)),
             pltpu.SemaphoreType.REGULAR((2,)),
         ],
         compiler_params=pltpu.CompilerParams(

time: 22.4 us -> 23.1 us (1.031)
  Pallas kernels: 21.6 us -> 22.4 us
    pallas_call x1, Pallas kernels: 20.5 us -> 21.3 us  [shards(): pl.pallas_call(kernel, out_shape=(jax.ShapeDtypeStruct((5, 8, 64, 128), f...]
where the time goes in v3:
time: 23.1 us; the launch traced here: 23 us
  Pallas kernels  22.4 us (97%)
  between operations  0.64 us (3%)
    pallas_call x1, Pallas kernels, shards(): pl.pallas_call(kernel, out_shape=(jax.ShapeDtypeStruct((5, 8, 64, 128), f...  21.3 us
    pallas_call x1, Pallas kernels, shards(): pl.pallas_call(functools.partial(write_out, cells), out_shape=(jax.ShapeD...  1.09 us

profile of v3, /device:TPU:1, one launch (start us, length us, event | category | flops | bytes accessed | tf_op | source)
XLA Modules:
  0.0 23.0 jit_solution(9712639399502302507)
XLA Ops:
  0.6 21.3 %remap.1 = (f32[5,8,64,128]{3,2,1,0:T(8,128)S(1)}, f32[1,128]{1,0:T(1,128)S(1)}) custom-call(f32[8,64,128]{2,1,0:T(8,128)} %density.1, f32[3,8,64,128]{3,2,1,0:T(8,128)} %momentum.1, f32[8,64,128]{2,1,0:T(8,128)} %energy.1, s32[3,8,64,128]{3,2,1,0:T(8,128)} %displacement.1, s32[6]{0:T(128)} %flags.1), custom_call_target="tpu_custom_call" | custom-call | tf_op jit(solution)/shard_map/remap/pallas_call | solution.py:590
  21.9 1.1 %write_out.1 = (f32[8,64,128]{2,1,0:T(8,128)}, f32[3,8,64,128]{3,2,1,0:T(8,128)}, f32[8,64,128]{2,1,0:T(8,128)}, f32[2]{0:T(128)}) custom-call(f32[5,8,64,128]{3,2,1,0:T(8,128)S(1)} %get-tuple-element.6.acc, f32[1,128]{1,0:T(1,128)S(1)} %get-tuple-element.7.grand), custom_call_target="tpu_custom_call" | custom-call | tf_op jit(solution)/shard_map/write_out/pallas_call | solution.py:635

commit v4 on v3

--- a/solution.py
+++ b/solution.py
@@ -116,7 +116,11 @@
         for dx in range(4)
         if dx or dc
     ]
-    stage_b = [along_yz(dy, dz) for dy in range(4) for dz in range(8) if dy or dz]
+    offsets_b = sorted(
+        [(dy, dz) for dy in range(4) for dz in range(8) if dy or dz],
+        key=lambda o: -min(o[0], 4 - o[0]) - min(o[1], 8 - o[1]),
+    )
+    stage_b = [along_yz(dy, dz) for dy, dz in offsets_b]
     along_y = [along_yz(dy, 0) for dy in (1, 2, 3)]
     steps = [-2, -1, 1, 2]
     late_step = [
@@ -224,6 +228,12 @@
     for copy in copies_a:
         copy.start()
 
+    @pl.when(jnp.logical_not(early))
+    def _():
+        greet_late(round_sem.at[0])
+        for peer in along_y:
+            greet(round_sem.at[0], peer)
+
     def remote(src, dst, send_sem, recv_sem, peer):
         return pltpu.make_async_remote_copy(
             src_ref=src,
@@ -268,27 +278,11 @@
     y_up = remote(yup, ylow, ys_sem.at[0], yr_sem.at[0], place(y=lax.rem(py + 1, ny)))
     y_down = remote(ydown, yhigh, ys_sem.at[1], yr_sem.at[1], place(y=lax.rem(py + ny - 1, ny)))
 
-    for back_step in (1, 2):
-
-        @pl.when(jnp.logical_and(level - back_step >= 0, level - back_step < EARLY))
-        def _():
-            greet(reply_sem.at[0], along_yz(0, 8 - back_step))
-
-    @pl.when(jnp.logical_not(early))
-    def _():
-        greet_late(round_sem.at[0])
-        for peer in along_y:
-            greet(round_sem.at[0], peer)
-
     @pl.when(jnp.logical_not(first[1]))
     def _():
         y_down.start()
 
-    @pl.when(early)
-    def _():
-        pl.semaphore_wait(reply_sem.at[0], 2)
-
-    @pl.when(jnp.logical_not(final[1]))
+    @pl.when(jnp.logical_not(jnp.logical_or(final[1], early)))
     def _():
         y_up.start()
 
@@ -323,12 +317,21 @@
     def _():
         z_down.start()
 
+    for back_step in (1, 2):
+
+        @pl.when(jnp.logical_and(level - back_step >= 0, level - back_step < EARLY))
+        def _():
+            greet(reply_sem.at[0], along_yz(0, 8 - back_step))
+
     for target in range(EARLY):
 
         @pl.when(target < level)
         def _():
             for dy in range(4):
-                greet(reply_sem.at[1], along_yz(dy, lax.rem(levels + target - level, levels)))
+                greet(
+                    reply_sem.at[jnp.where(early, 2, 1)],
+                    along_yz(dy, lax.rem(levels + target - level, levels)),
+                )
 
     scale_y = jnp.where(
         jnp.logical_or(rows < 2, rows == 63), 0.0, STEP
@@ -364,28 +367,54 @@
             acc[f, x] = (value + (flux - pltpu.roll(flux, 63, 0))) + change_z
         return carry
 
-    lax.fori_loop(0, 2, planes, 0)
-
-    @pl.when(jnp.logical_not(early))
+    lax.fori_loop(0, 3, planes, 0)
+
+    late = jnp.logical_not(early)
+
+    @pl.when(late)
     def _():
         pl.semaphore_wait(round_sem.at[0], len(along_y) + late_steps)
         greet_late(round_sem.at[1])
         for peer in along_y:
             greet(round_sem.at[1], peer)
 
-    lax.fori_loop(2, 4, planes, 0)
-
     for copy in copies_a:
         copy.wait_recv()
     part[1] = part[0] + jnp.sum(slots_a[...], axis=0)
 
-    @pl.when(jnp.logical_not(early))
+    def far(dz):
+        other = lax.rem(level + dz, levels)
+        return jnp.logical_and(other >= EARLY, jnp.abs(other - level) > 2)
+
+    @pl.when(late)
+    def _():
+        for (dy, dz), copy in zip(offsets_b, copies_b):
+            if dz in (3, 4, 5):
+                pl.when(jnp.logical_not(far(dz)))(copy.start)
+            else:
+                copy.start()
+
+    @pl.when(early)
+    def _():
+        pl.semaphore_wait(reply_sem.at[0], 2)
+        y_up.start()
+
+        @pl.when(level < EARLY - 1)
+        def _():
+            pl.semaphore_wait(reply_sem.at[2], 4 * (EARLY - 1 - level))
+
+        for (dy, dz), copy in zip(offsets_b, copies_b):
+            if dz in (0, 1, 2, 6, 7):
+                pl.when(lax.rem(level + dz, levels) < EARLY)(copy.start)
+
+    lax.fori_loop(3, 8, planes, 0)
+
+    @pl.when(late)
     def _():
         pl.semaphore_wait(round_sem.at[1], len(along_y) + late_steps)
-        for copy in copies_b:
-            copy.start()
-
-    lax.fori_loop(4, 8, planes, 0)
+        for (dy, dz), copy in zip(offsets_b, copies_b):
+            if dz in (3, 4, 5):
+                pl.when(far(dz))(copy.start)
 
     @pl.when(jnp.logical_not(first[1]))
     def _():
@@ -470,9 +499,10 @@
 
     @pl.when(early)
     def _():
-        pl.semaphore_wait(reply_sem.at[1], 4 * (levels - 1 - level))
-        for copy in copies_b:
-            copy.start()
+        pl.semaphore_wait(reply_sem.at[1], 4 * (levels - EARLY))
+        for (dy, dz), copy in zip(offsets_b, copies_b):
+            if dz:
+                pl.when(lax.rem(level + dz, levels) >= EARLY)(copy.start)
 
     @pl.when(jnp.logical_not(final[0]))
     def _():
@@ -527,11 +557,7 @@
 
         lax.fori_loop(0, 8, tile, 0)
 
-    for copy in copies_b:
-        copy.wait_recv()
-    grand[...] = part[1] + jnp.sum(slots_b[...], axis=0)
-
-    for copy in copies_a + copies_b:
+    for copy in copies_a:
         copy.wait_send()
 
     @pl.when(jnp.logical_not(first[0]))
@@ -558,6 +584,12 @@
         @pl.when(jnp.logical_not(first[0]))
         def _():
             down_copies[f].wait_send()
+
+    for copy in copies_b:
+        copy.wait_send()
+    for copy in copies_b:
+        copy.wait_recv()
+    grand[...] = part[1] + jnp.sum(slots_b[...], axis=0)
 
 
 def write_out(cells, acc, grand, new_density, new_momentum, new_energy, totals, pair, sem):
@@ -625,7 +657,7 @@
             pltpu.SemaphoreType.DMA((38,)),
             pltpu.SemaphoreType.DMA((38,)),
             pltpu.SemaphoreType.REGULAR((2,)),
-            pltpu.SemaphoreType.REGULAR((2,)),
+            pltpu.SemaphoreType.REGULAR((3,)),
         ],
         compiler_params=pltpu.CompilerParams(
             collective_id=0, has_side_effects=True, vmem_limit_bytes=16 * 2**20

time: 23.1 us -> 21 us (0.909)
  Pallas kernels: 22.4 us -> 20.2 us
    pallas_call x1, Pallas kernels: 21.3 us -> 19.1 us  [shards(): pl.pallas_call(kernel, out_shape=(jax.ShapeDtypeStruct((5, 8, 64, 128), f...]
where the time goes in v4:
time: 21 us; the launch traced here: 20.8 us
  Pallas kernels  20.2 us (96%)
  between operations  0.64 us (3%)
    pallas_call x1, Pallas kernels, shards(): pl.pallas_call(kernel, out_shape=(jax.ShapeDtypeStruct((5, 8, 64, 128), f...  19.1 us
    pallas_call x1, Pallas kernels, shards(): pl.pallas_call(functools.partial(write_out, cells), out_shape=(jax.ShapeD...  1.09 us

profile of v4, /device:TPU:1, one launch (start us, length us, event | category | flops | bytes accessed | tf_op | source)
XLA Modules:
  0.0 20.8 jit_solution(8775815537119595700)
XLA Ops:
  0.6 19.1 %remap.1 = (f32[5,8,64,128]{3,2,1,0:T(8,128)S(1)}, f32[1,128]{1,0:T(1,128)S(1)}) custom-call(f32[8,64,128]{2,1,0:T(8,128)} %density.1, f32[3,8,64,128]{3,2,1,0:T(8,128)} %momentum.1, f32[8,64,128]{2,1,0:T(8,128)} %energy.1, s32[3,8,64,128]{3,2,1,0:T(8,128)} %displacement.1, s32[6]{0:T(128)} %flags.1), custom_call_target="tpu_custom_call" | custom-call | tf_op jit(solution)/shard_map/remap/pallas_call | solution.py:622
  19.8 1.1 %write_out.1 = (f32[8,64,128]{2,1,0:T(8,128)}, f32[3,8,64,128]{3,2,1,0:T(8,128)}, f32[8,64,128]{2,1,0:T(8,128)}, f32[2]{0:T(128)}) custom-call(f32[5,8,64,128]{3,2,1,0:T(8,128)S(1)} %get-tuple-element.6.acc, f32[1,128]{1,0:T(1,128)S(1)} %get-tuple-element.7.grand), custom_call_target="tpu_custom_call" | custom-call | tf_op jit(solution)/shard_map/write_out/pallas_call | solution.py:667

commit v5 on v4

--- a/solution.py
+++ b/solution.py
@@ -44,8 +44,7 @@
     flag,
     vx,
     gx_w,
-    xlow,
-    xhigh,
+    xhalo,
     xface,
     yup,
     ydown,
@@ -74,20 +73,17 @@
     nx, ny, nz = lax.axis_size("gx"), lax.axis_size("gy"), lax.axis_size("gz")
     core = pz % 2
     zl = (pz // 2) % 2
-    field_in = [density, momentum.at[0], momentum.at[1], momentum.at[2], energy]
-
-    flag_copy = pltpu.make_async_copy(flags, flag, load_sem.at[8])
+    flag_copy = pltpu.make_async_copy(flags, flag, load_sem.at[0])
     flag_copy.start()
-    loads = [pltpu.make_async_copy(field_in[f], q.at[f], load_sem.at[f]) for f in range(5)]
-    disp_loads = [
-        pltpu.make_async_copy(displacement.at[a], disp.at[a], load_sem.at[5 + a]) for a in range(3)
-    ]
-    loads[0].start()
-    loads[4].start()
-    for copy in disp_loads:
-        copy.start()
-    for f in (1, 2, 3):
-        loads[f].start()
+    pltpu.make_async_copy(density, q.at[0], load_sem.at[1]).start()
+    pltpu.make_async_copy(energy, q.at[1], load_sem.at[1]).start()
+    disp_load = pltpu.make_async_copy(displacement, disp, load_sem.at[2])
+    disp_load.start()
+    momentum_load = pltpu.make_async_copy(momentum, q.at[pl.ds(2, 3)], load_sem.at[3])
+    momentum_load.start()
+
+    def wait_bytes(of, sem):
+        pltpu.make_async_copy(of, of, sem).wait()
 
     def place(x=None, y=None, z=None):
         target = {}
@@ -116,11 +112,6 @@
         for dx in range(4)
         if dx or dc
     ]
-    offsets_b = sorted(
-        [(dy, dz) for dy in range(4) for dz in range(8) if dy or dz],
-        key=lambda o: -min(o[0], 4 - o[0]) - min(o[1], 8 - o[1]),
-    )
-    stage_b = [along_yz(dy, dz) for dy, dz in offsets_b]
     along_y = [along_yz(dy, 0) for dy in (1, 2, 3)]
     steps = [-2, -1, 1, 2]
     late_step = [
@@ -159,10 +150,8 @@
         greet_late(barrier)
 
     flag_copy.wait()
-    loads[0].wait()
-    loads[4].wait()
-    for copy in disp_loads:
-        copy.wait()
+    wait_bytes(q.at[pl.ds(0, 2)], load_sem.at[1])
+    disp_load.wait()
 
     flag_open = [flag[i].astype(jnp.float32) for i in range(6)]
     first = [px == 0, py == 0, pz == 0]
@@ -185,11 +174,11 @@
             + weight_y * disp[1, x].astype(jnp.float32)
             + weight_z * disp[2, x].astype(jnp.float32)
         )
-        return (sums[0] + fold(q[0, x] * weight), sums[1] + fold(q[4, x] * weight))
+        return (sums[0] + fold(q[0, x] * weight), sums[1] + fold(q[1, x] * weight))
 
     weight_low = gain[0] * disp[0, 0].astype(jnp.float32)
     weight_high = loss[0] * disp[0, 7].astype(jnp.float32)
-    sums = tuple(fold(q[f, 0] * weight_low + q[f, 7] * weight_high) for f in (0, 4))
+    sums = tuple(fold(q[f, 0] * weight_low + q[f, 7] * weight_high) for f in (0, 1))
     sums = lax.fori_loop(0, 8, plane_sum, sums)
     lane1 = lax.broadcasted_iota(jnp.int32, (1, 128), 1)
 
@@ -199,8 +188,7 @@
         return jnp.where(lane1 < 64, low + pltpu.roll(low, 64, 1), high + pltpu.roll(high, 64, 1))
 
     part[0] = halves(*sums)
-    for f in (1, 2, 3):
-        loads[f].wait()
+    momentum_load.wait()
 
     greeted = (
         len(stage_a)
@@ -210,21 +198,26 @@
     )
     pl.semaphore_wait(barrier, greeted)
 
-    def total_copies(stage, peers, slots, base):
+    offsets_b = sorted(
+        [(dy, dz) for dy in range(4) for dz in range(8) if dy or dz],
+        key=lambda o: -min(o[0], 4 - o[0]) - min(o[1], 8 - o[1]),
+    )
+    stage_b = [along_yz(dy, dz) for dy, dz in offsets_b]
+    def total_copies(stage, peers, slots):
         return [
             pltpu.make_async_remote_copy(
                 src_ref=part.at[stage],
                 dst_ref=slots.at[i],
-                send_sem=ts_sem.at[base + i],
-                recv_sem=tr_sem.at[base + i],
+                send_sem=ts_sem.at[stage],
+                recv_sem=tr_sem.at[stage],
                 device_id=peer,
                 device_id_type=MESH,
             )
             for i, peer in enumerate(peers)
         ]
 
-    copies_a = total_copies(0, stage_a, slots_a, 0)
-    copies_b = total_copies(1, stage_b, slots_b, 7)
+    copies_a = total_copies(0, stage_a, slots_a)
+    copies_b = total_copies(1, stage_b, slots_b)
     for copy in copies_a:
         copy.start()
 
@@ -246,12 +239,12 @@
 
     x_next = place(x=lax.rem(px + 1, nx))
     x_prev = place(x=lax.rem(px + nx - 1, nx))
-    face_copy = remote(disp.at[0, 0], xface, xs_sem.at[10], xr_sem.at[10], x_prev)
+    face_copy = remote(disp.at[0, 0], xface, xs_sem.at[2], xr_sem.at[5], x_prev)
     up_copies = [
-        remote(q.at[f, pl.ds(6, 2)], xlow.at[f], xs_sem.at[f], xr_sem.at[f], x_next) for f in range(5)
+        remote(q.at[f, pl.ds(6, 2)], xhalo.at[f, 0], xs_sem.at[0], xr_sem.at[f], x_next) for f in range(5)
     ]
     down_copies = [
-        remote(q.at[f, pl.ds(0, 2)], xhigh.at[f], xs_sem.at[5 + f], xr_sem.at[5 + f], x_prev)
+        remote(q.at[f, pl.ds(0, 2)], xhalo.at[f, 1], xs_sem.at[1], xr_sem.at[f], x_prev)
         for f in range(5)
     ]
 
@@ -378,8 +371,7 @@
         for peer in along_y:
             greet(round_sem.at[1], peer)
 
-    for copy in copies_a:
-        copy.wait_recv()
+    wait_bytes(slots_a, tr_sem.at[0])
     part[1] = part[0] + jnp.sum(slots_a[...], axis=0)
 
     def far(dz):
@@ -519,24 +511,25 @@
         vx[i] = v
         gx_w[i] = half_weight(v)
 
+    inner = jnp.logical_not(jnp.logical_or(first[0], final[0]))
     edge_lanes = jnp.logical_or(lane8 < 2, lane8 > 125)
     for f in range(5):
 
-        @pl.when(jnp.logical_not(first[0]))
-        def _():
-            up_copies[f].wait_recv()
-
-        @pl.when(jnp.logical_not(final[0]))
-        def _():
-            down_copies[f].wait_recv()
+        @pl.when(inner)
+        def _():
+            wait_bytes(xhalo.at[f], xr_sem.at[f])
+
+        @pl.when(jnp.logical_not(inner))
+        def _():
+            wait_bytes(xhalo.at[f, 0], xr_sem.at[f])
 
         def tile(t, carry):
             part_rows = pl.ds(pl.multiple_of(t * 8, 8), 8)
             own = [q[f, i, part_rows] for i in range(8)]
             cell = (
-                [jnp.where(first[0], own[0], xlow[f, r, part_rows]) for r in range(2)]
+                [jnp.where(first[0], own[0], xhalo[f, 0, r, part_rows]) for r in range(2)]
                 + own
-                + [jnp.where(final[0], own[7], xhigh[f, r, part_rows]) for r in range(2)]
+                + [jnp.where(final[0], own[7], xhalo[f, 1, r, part_rows]) for r in range(2)]
             )
             diff = [cell[i + 1] - cell[i] for i in range(11)]
             slope = [minmod(diff[i], diff[i + 1]) for i in range(10)]
@@ -557,8 +550,7 @@
 
         lax.fori_loop(0, 8, tile, 0)
 
-    for copy in copies_a:
-        copy.wait_send()
+    wait_bytes(slots_a, ts_sem.at[0])
 
     @pl.when(jnp.logical_not(first[0]))
     def _():
@@ -575,39 +567,33 @@
         def _():
             copy.wait_send()
 
-    for f in range(5):
-
-        @pl.when(jnp.logical_not(final[0]))
-        def _():
-            up_copies[f].wait_send()
-
-        @pl.when(jnp.logical_not(first[0]))
-        def _():
-            down_copies[f].wait_send()
-
-    for copy in copies_b:
-        copy.wait_send()
-    for copy in copies_b:
-        copy.wait_recv()
+    @pl.when(jnp.logical_not(final[0]))
+    def _():
+        wait_bytes(xhalo.at[:, 0], xs_sem.at[0])
+
+    @pl.when(jnp.logical_not(first[0]))
+    def _():
+        wait_bytes(xhalo.at[:, 1], xs_sem.at[1])
+
+    wait_bytes(slots_b, ts_sem.at[1])
+    wait_bytes(slots_b, tr_sem.at[1])
     grand[...] = part[1] + jnp.sum(slots_b[...], axis=0)
 
 
 def write_out(cells, acc, grand, new_density, new_momentum, new_energy, totals, pair, sem):
     stores = [
         pltpu.make_async_copy(acc.at[0], new_density, sem.at[0]),
-        pltpu.make_async_copy(acc.at[pl.ds(1, 3)], new_momentum, sem.at[1]),
-        pltpu.make_async_copy(acc.at[4], new_energy, sem.at[2]),
-    ]
+        pltpu.make_async_copy(acc.at[1], new_energy, sem.at[0]),
+    ] + [pltpu.make_async_copy(acc.at[2 + c], new_momentum.at[c], sem.at[0]) for c in range(3)]
     for store in stores:
         store.start()
     lane1 = lax.broadcasted_iota(jnp.int32, (1, 128), 1)
     both = grand[...]
     pair[0] = jnp.sum(jnp.where(lane1 < 64, both, 0.0)) / cells
     pair[1] = jnp.sum(jnp.where(lane1 < 64, 0.0, both)) / cells
-    last = pltpu.make_async_copy(pair, totals, sem.at[3])
+    last = pltpu.make_async_copy(pair, totals, sem.at[1])
     last.start()
-    for store in stores:
-        store.wait()
+    pltpu.make_async_copy(acc, acc, sem.at[0]).wait()
     last.wait()
 
 
@@ -633,8 +619,7 @@
             pltpu.SMEM((6,), i32),
             pltpu.VMEM((9, 64, 128), f32),
             pltpu.VMEM((9, 64, 128), f32),
-            pltpu.VMEM((5, 2, 64, 128), f32),
-            pltpu.VMEM((5, 2, 64, 128), f32),
+            pltpu.VMEM((5, 2, 2, 64, 128), f32),
             pltpu.VMEM((64, 128), i32),
             pltpu.VMEM((10, 8, 128), f32),
             pltpu.VMEM((11, 8, 128), f32),
@@ -647,15 +632,15 @@
             pltpu.VMEM((2, 1, 128), f32),
             pltpu.VMEM((7, 1, 128), f32),
             pltpu.VMEM((31, 1, 128), f32),
-            pltpu.SemaphoreType.DMA((9,)),
-            pltpu.SemaphoreType.DMA((11,)),
-            pltpu.SemaphoreType.DMA((11,)),
+            pltpu.SemaphoreType.DMA((4,)),
+            pltpu.SemaphoreType.DMA((3,)),
+            pltpu.SemaphoreType.DMA((6,)),
             pltpu.SemaphoreType.DMA((2,)),
             pltpu.SemaphoreType.DMA((2,)),
             pltpu.SemaphoreType.DMA((2,)),
             pltpu.SemaphoreType.DMA((2,)),
-            pltpu.SemaphoreType.DMA((38,)),
-            pltpu.SemaphoreType.DMA((38,)),
+            pltpu.SemaphoreType.DMA((2,)),
+            pltpu.SemaphoreType.DMA((2,)),
             pltpu.SemaphoreType.REGULAR((2,)),
             pltpu.SemaphoreType.REGULAR((3,)),
         ],
@@ -674,7 +659,7 @@
         ),
         in_specs=[local, local],
         out_specs=[anywhere] * 4,
-        scratch_shapes=[pltpu.SMEM((2,), f32), pltpu.SemaphoreType.DMA((4,))],
+        scratch_shapes=[pltpu.SMEM((2,), f32), pltpu.SemaphoreType.DMA((2,))],
         compiler_params=pltpu.CompilerParams(vmem_limit_bytes=4 * 2**20),
         name="write_out",
     )(acc, grand)

time: 21 us -> 19.9 us (0.948)
  Pallas kernels: 20.2 us -> 19.2 us
    pallas_call x1, Pallas kernels: 19.1 us -> 18.1 us  [shards(): pl.pallas_call(kernel, out_shape=(jax.ShapeDtypeStruct((5, 8, 64, 128), f...]
where the time goes in v5:
time: 19.9 us; the launch traced here: 19.8 us
  Pallas kernels  19.2 us (96%)
  between operations  0.64 us (3%)
    pallas_call x1, Pallas kernels, shards(): pl.pallas_call(kernel, out_shape=(jax.ShapeDtypeStruct((5, 8, 64, 128), f...  18.1 us
    pallas_call x1, Pallas kernels, shards(): pl.pallas_call(functools.partial(write_out, cells), out_shape=(jax.ShapeD...  1.07 us

profile of v5, /device:TPU:1, one launch (start us, length us, event | category | flops | bytes accessed | tf_op | source)
XLA Modules:
  0.0 19.8 jit_solution(7248914884737393588)
XLA Ops:
  0.6 18.1 %remap.1 = (f32[5,8,64,128]{3,2,1,0:T(8,128)S(1)}, f32[1,128]{1,0:T(1,128)S(1)}) custom-call(f32[8,64,128]{2,1,0:T(8,128)} %density.1, f32[3,8,64,128]{3,2,1,0:T(8,128)} %momentum.1, f32[8,64,128]{2,1,0:T(8,128)} %energy.1, s32[3,8,64,128]{3,2,1,0:T(8,128)} %displacement.1, s32[6]{0:T(128)} %flags.1), custom_call_target="tpu_custom_call" | custom-call | tf_op jit(solution)/shard_map/remap/pallas_call | solution.py:608
  18.8 1.1 %write_out.1 = (f32[8,64,128]{2,1,0:T(8,128)}, f32[3,8,64,128]{3,2,1,0:T(8,128)}, f32[8,64,128]{2,1,0:T(8,128)}, f32[2]{0:T(128)}) custom-call(f32[5,8,64,128]{3,2,1,0:T(8,128)S(1)} %get-tuple-element.6.acc, f32[1,128]{1,0:T(1,128)S(1)} %get-tuple-element.7.grand), custom_call_target="tpu_custom_call" | custom-call | tf_op jit(solution)/shard_map/write_out/pallas_call | solution.py:652

commit v6 on v5

--- a/solution.py
+++ b/solution.py
@@ -203,30 +203,6 @@
         key=lambda o: -min(o[0], 4 - o[0]) - min(o[1], 8 - o[1]),
     )
     stage_b = [along_yz(dy, dz) for dy, dz in offsets_b]
-    def total_copies(stage, peers, slots):
-        return [
-            pltpu.make_async_remote_copy(
-                src_ref=part.at[stage],
-                dst_ref=slots.at[i],
-                send_sem=ts_sem.at[stage],
-                recv_sem=tr_sem.at[stage],
-                device_id=peer,
-                device_id_type=MESH,
-            )
-            for i, peer in enumerate(peers)
-        ]
-
-    copies_a = total_copies(0, stage_a, slots_a)
-    copies_b = total_copies(1, stage_b, slots_b)
-    for copy in copies_a:
-        copy.start()
-
-    @pl.when(jnp.logical_not(early))
-    def _():
-        greet_late(round_sem.at[0])
-        for peer in along_y:
-            greet(round_sem.at[0], peer)
-
     def remote(src, dst, send_sem, recv_sem, peer):
         return pltpu.make_async_remote_copy(
             src_ref=src,
@@ -236,6 +212,43 @@
             device_id=peer,
             device_id_type=MESH,
         )
+
+    copies_a = [
+        remote(part.at[0], slots_a.at[i], ts_sem.at[0], tr_sem.at[0], peer)
+        for i, peer in enumerate(stage_a)
+    ]
+    slot = level * 4 + pz // 4
+    arrival = tr_sem.at[jnp.where(early, 1, 2)]
+    copies_b = [
+        remote(part.at[1], slots_b.at[slot], ts_sem.at[1], arrival, peer) for peer in stage_b
+    ]
+    for copy in copies_a:
+        copy.start()
+
+    @pl.when(jnp.logical_not(early))
+    def _():
+        greet_late(round_sem.at[0])
+        for peer in along_y:
+            greet(round_sem.at[0], peer)
+
+    for back_step in (1, 2):
+
+        @pl.when(jnp.logical_and(level - back_step >= 0, level - back_step < EARLY))
+        def _():
+            greet(reply_sem.at[0], along_yz(0, 8 - back_step))
+
+    @pl.when(early)
+    def _():
+        for target in range(EARLY - 1):
+
+            @pl.when(target < level)
+            def _():
+                for dy in range(4):
+                    greet(reply_sem.at[2], along_yz(dy, lax.rem(levels + target - level, levels)))
+
+    @pl.when(jnp.logical_not(early))
+    def _():
+        greet(reply_sem.at[1], along_yz(0, lax.rem(levels + EARLY - 1 - level, levels)))
 
     x_next = place(x=lax.rem(px + 1, nx))
     x_prev = place(x=lax.rem(px + nx - 1, nx))
@@ -309,22 +322,6 @@
     @pl.when(jnp.logical_not(first[2]))
     def _():
         z_down.start()
-
-    for back_step in (1, 2):
-
-        @pl.when(jnp.logical_and(level - back_step >= 0, level - back_step < EARLY))
-        def _():
-            greet(reply_sem.at[0], along_yz(0, 8 - back_step))
-
-    for target in range(EARLY):
-
-        @pl.when(target < level)
-        def _():
-            for dy in range(4):
-                greet(
-                    reply_sem.at[jnp.where(early, 2, 1)],
-                    along_yz(dy, lax.rem(levels + target - level, levels)),
-                )
 
     scale_y = jnp.where(
         jnp.logical_or(rows < 2, rows == 63), 0.0, STEP
@@ -372,7 +369,9 @@
             greet(round_sem.at[1], peer)
 
     wait_bytes(slots_a, tr_sem.at[0])
-    part[1] = part[0] + jnp.sum(slots_a[...], axis=0)
+    group = part[0] + jnp.sum(slots_a[...], axis=0)
+    part[1] = group
+    slots_b[slot] = group
 
     def far(dz):
         other = lax.rem(level + dz, levels)
@@ -388,18 +387,21 @@
 
     @pl.when(early)
     def _():
-        pl.semaphore_wait(reply_sem.at[0], 2)
-        y_up.start()
+        for (dy, dz), copy in zip(offsets_b, copies_b):
+            if dz in (0, 6, 7):
+                pl.when(level + dz >= (levels if dz else 0))(copy.start)
 
         @pl.when(level < EARLY - 1)
         def _():
             pl.semaphore_wait(reply_sem.at[2], 4 * (EARLY - 1 - level))
 
         for (dy, dz), copy in zip(offsets_b, copies_b):
-            if dz in (0, 1, 2, 6, 7):
-                pl.when(lax.rem(level + dz, levels) < EARLY)(copy.start)
-
-    lax.fori_loop(3, 8, planes, 0)
+            if dz in (1, 2):
+                pl.when(level + dz < EARLY)(copy.start)
+        pl.semaphore_wait(reply_sem.at[0], 2)
+        y_up.start()
+
+    lax.fori_loop(3, 6, planes, 0)
 
     @pl.when(late)
     def _():
@@ -407,6 +409,8 @@
         for (dy, dz), copy in zip(offsets_b, copies_b):
             if dz in (3, 4, 5):
                 pl.when(far(dz))(copy.start)
+
+    lax.fori_loop(6, 8, planes, 0)
 
     @pl.when(jnp.logical_not(first[1]))
     def _():
@@ -489,12 +493,19 @@
                 ),
             )
 
-    @pl.when(early)
-    def _():
-        pl.semaphore_wait(reply_sem.at[1], 4 * (levels - EARLY))
-        for (dy, dz), copy in zip(offsets_b, copies_b):
-            if dz:
-                pl.when(lax.rem(level + dz, levels) >= EARLY)(copy.start)
+    last_early = level == EARLY - 1
+    copies_c = [
+        remote(part.at[2], slots_b.at[0], ts_sem.at[2], tr_sem.at[1], along_yz(0, dz))
+        for dz in range(1, 6)
+    ]
+
+    @pl.when(last_early)
+    def _():
+        wait_bytes(slots_b.at[pl.ds(0, 4 * EARLY - 1)], tr_sem.at[1])
+        part[2] = jnp.sum(slots_b[: 4 * EARLY], axis=0)
+        pl.semaphore_wait(reply_sem.at[1], levels - EARLY)
+        for copy in copies_c:
+            copy.start()
 
     @pl.when(jnp.logical_not(final[0]))
     def _():
@@ -575,9 +586,31 @@
     def _():
         wait_bytes(xhalo.at[:, 1], xs_sem.at[1])
 
-    wait_bytes(slots_b, ts_sem.at[1])
-    wait_bytes(slots_b, tr_sem.at[1])
-    grand[...] = part[1] + jnp.sum(slots_b[...], axis=0)
+    @pl.when(early)
+    def _():
+        wait_bytes(slots_b.at[pl.ds(0, 4 * EARLY - 1)], ts_sem.at[1])
+        wait_bytes(slots_b.at[pl.ds(0, 4 * (8 - EARLY))], tr_sem.at[2])
+
+    @pl.when(level < EARLY - 1)
+    def _():
+        wait_bytes(slots_b.at[pl.ds(0, 4 * EARLY - 1)], tr_sem.at[1])
+
+    @pl.when(last_early)
+    def _():
+        wait_bytes(slots_b.at[pl.ds(0, 5)], ts_sem.at[2])
+
+    @pl.when(late)
+    def _():
+        wait_bytes(slots_b.at[pl.ds(0, 31)], ts_sem.at[1])
+        wait_bytes(slots_b.at[pl.ds(0, 1)], tr_sem.at[1])
+        wait_bytes(slots_b.at[pl.ds(0, 4 * (8 - EARLY) - 1)], tr_sem.at[2])
+
+    others = jnp.sum(slots_b[1 : 4 * EARLY], axis=0)
+    grand[...] = (
+        slots_b[0]
+        + jnp.where(early, others, 0.0)
+        + jnp.sum(slots_b[4 * EARLY :], axis=0)
+    )
 
 
 def write_out(cells, acc, grand, new_density, new_momentum, new_energy, totals, pair, sem):
@@ -629,9 +662,9 @@
             pltpu.VMEM((12, 8, 128), f32),
             pltpu.VMEM((12, 8, 128), f32),
             pltpu.VMEM((10, 8, 128), f32),
-            pltpu.VMEM((2, 1, 128), f32),
+            pltpu.VMEM((3, 1, 128), f32),
             pltpu.VMEM((7, 1, 128), f32),
-            pltpu.VMEM((31, 1, 128), f32),
+            pltpu.VMEM((32, 1, 128), f32),
             pltpu.SemaphoreType.DMA((4,)),
             pltpu.SemaphoreType.DMA((3,)),
             pltpu.SemaphoreType.DMA((6,)),
@@ -639,8 +672,8 @@
             pltpu.SemaphoreType.DMA((2,)),
             pltpu.SemaphoreType.DMA((2,)),
             pltpu.SemaphoreType.DMA((2,)),
-            pltpu.SemaphoreType.DMA((2,)),
-            pltpu.SemaphoreType.DMA((2,)),
+            pltpu.SemaphoreType.DMA((3,)),
+            pltpu.SemaphoreType.DMA((3,)),
             pltpu.SemaphoreType.REGULAR((2,)),
             pltpu.SemaphoreType.REGULAR((3,)),
         ],

time: 19.9 us -> 19.8 us (level)
  no operation moved by 1% of the time
where the time goes in v6:
time: 19.8 us; the launch traced here: 19.7 us
  Pallas kernels  19.1 us (96%)
  between operations  0.64 us (3%)
    pallas_call x1, Pallas kernels, shards(): pl.pallas_call(kernel, out_shape=(jax.ShapeDtypeStruct((5, 8, 64, 128), f...  18 us
    pallas_call x1, Pallas kernels, shards(): pl.pallas_call(functools.partial(write_out, cells), out_shape=(jax.ShapeD...  1.07 us

profile of v6, /device:TPU:1, one launch (start us, length us, event | category | flops | bytes accessed | tf_op | source)
XLA Modules:
  0.0 19.7 jit_solution(3371309631251020884)
XLA Ops:
  0.6 18.0 %remap.1 = (f32[5,8,64,128]{3,2,1,0:T(8,128)S(1)}, f32[1,128]{1,0:T(1,128)S(1)}) custom-call(f32[8,64,128]{2,1,0:T(8,128)} %density.1, f32[3,8,64,128]{3,2,1,0:T(8,128)} %momentum.1, f32[8,64,128]{2,1,0:T(8,128)} %energy.1, s32[3,8,64,128]{3,2,1,0:T(8,128)} %displacement.1, s32[6]{0:T(128)} %flags.1), custom_call_target="tpu_custom_call" | custom-call | tf_op jit(solution)/shard_map/remap/pallas_call | solution.py:641
  18.6 1.1 %write_out.1 = (f32[8,64,128]{2,1,0:T(8,128)}, f32[3,8,64,128]{3,2,1,0:T(8,128)}, f32[8,64,128]{2,1,0:T(8,128)}, f32[2]{0:T(128)}) custom-call(f32[5,8,64,128]{3,2,1,0:T(8,128)S(1)} %get-tuple-element.6.acc, f32[1,128]{1,0:T(1,128)S(1)} %get-tuple-element.7.grand), custom_call_target="tpu_custom_call" | custom-call | tf_op jit(solution)/shard_map/write_out/pallas_call | solution.py:685

commit v7 on v6

--- a/solution.py
+++ b/solution.py
@@ -57,6 +57,7 @@
     part,
     slots_a,
     slots_b,
+    slots_d,
     load_sem,
     xs_sem,
     xr_sem,
@@ -73,15 +74,6 @@
     nx, ny, nz = lax.axis_size("gx"), lax.axis_size("gy"), lax.axis_size("gz")
     core = pz % 2
     zl = (pz // 2) % 2
-    flag_copy = pltpu.make_async_copy(flags, flag, load_sem.at[0])
-    flag_copy.start()
-    pltpu.make_async_copy(density, q.at[0], load_sem.at[1]).start()
-    pltpu.make_async_copy(energy, q.at[1], load_sem.at[1]).start()
-    disp_load = pltpu.make_async_copy(displacement, disp, load_sem.at[2])
-    disp_load.start()
-    momentum_load = pltpu.make_async_copy(momentum, q.at[pl.ds(2, 3)], load_sem.at[3])
-    momentum_load.start()
-
     def wait_bytes(of, sem):
         pltpu.make_async_copy(of, of, sem).wait()
 
@@ -108,8 +100,8 @@
 
     stage_a = [
         place(x=lax.rem(px + dx, nx), z=pz + dc * (1 - 2 * core))
+        for dx in (2, 1, 3, 0)
         for dc in range(2)
-        for dx in range(4)
         if dx or dc
     ]
     along_y = [along_yz(dy, 0) for dy in (1, 2, 3)]
@@ -132,9 +124,38 @@
     for peer in stage_a + along_y:
         greet(barrier, peer)
 
+    flag_copy = pltpu.make_async_copy(flags, flag, load_sem.at[0])
+    flag_copy.start()
+    pltpu.make_async_copy(density, q.at[0], load_sem.at[1]).start()
+    pltpu.make_async_copy(energy, q.at[1], load_sem.at[1]).start()
+    disp_load = pltpu.make_async_copy(displacement, disp, load_sem.at[2])
+    disp_load.start()
+    momentum_load = pltpu.make_async_copy(momentum, q.at[pl.ds(2, 3)], load_sem.at[3])
+    momentum_load.start()
+
     @pl.when(has_across)
     def _():
         greet(barrier, across)
+
+    in_column = jnp.logical_and(px == 0, core == 1)
+    root = jnp.logical_and(in_column, jnp.logical_and(level == 0, pz < 2))
+
+    @pl.when(root)
+    def _():
+        def greet_group(k, carry):
+            t = lax.rem(k // 4 + EARLY, 8)
+            y = lax.rem(k, 4)
+            z = 4 * y + 2 * lax.rem(t, 2)
+            for x in range(4):
+                for c in range(2):
+                    peer = place(x=x, y=t // 2, z=z + c)
+                    if x or not c:
+                        greet(barrier, peer)
+                    else:
+                        pl.when(t + y > 0)(functools.partial(greet, barrier, peer))
+            return carry
+
+        lax.fori_loop(0, 32, greet_group, 0)
 
     @pl.when(early)
     def _():
@@ -194,15 +215,12 @@
         len(stage_a)
         + len(along_y)
         + has_across.astype(jnp.int32)
+        + 1
+        - root.astype(jnp.int32)
         + jnp.where(early, 4 * level, 4 * EARLY + late_steps)
     )
     pl.semaphore_wait(barrier, greeted)
 
-    offsets_b = sorted(
-        [(dy, dz) for dy in range(4) for dz in range(8) if dy or dz],
-        key=lambda o: -min(o[0], 4 - o[0]) - min(o[1], 8 - o[1]),
-    )
-    stage_b = [along_yz(dy, dz) for dy, dz in offsets_b]
     def remote(src, dst, send_sem, recv_sem, peer):
         return pltpu.make_async_remote_copy(
             src_ref=src,
@@ -219,9 +237,37 @@
     ]
     slot = level * 4 + pz // 4
     arrival = tr_sem.at[jnp.where(early, 1, 2)]
+    me_y = pz // 4
+    base_z = pz - 4 * me_y - 2 * zl
+    places = [(t, y) for t in range(8) for y in (0, 1, 3, 2)]
     copies_b = [
-        remote(part.at[1], slots_b.at[slot], ts_sem.at[1], arrival, peer) for peer in stage_b
+        remote(
+            part.at[1],
+            slots_b.at[slot],
+            ts_sem.at[1],
+            arrival,
+            place(y=t // 2, z=base_z + 4 * y + 2 * (t % 2)),
+        )
+        for t, y in places
     ]
+
+    def send_b(wanted):
+        for (t, y), copy in zip(places, copies_b):
+            ok = wanted(t)
+            if ok is not None:
+                other = jnp.logical_or(level != t, me_y != y)
+                if not (t or y):
+                    other = jnp.logical_and(other, jnp.logical_not(in_column))
+                pl.when(jnp.logical_and(ok, other))(copy.start)
+    index = (px * ny + py) * nz + pz
+    to_root = remote(
+        part.at[0], slots_d.at[index], ts_sem.at[3], tr_sem.at[3], place(x=0, y=0, z=1)
+    )
+
+    @pl.when(jnp.logical_not(root))
+    def _():
+        to_root.start()
+
     for copy in copies_a:
         copy.start()
 
@@ -373,31 +419,24 @@
     part[1] = group
     slots_b[slot] = group
 
-    def far(dz):
-        other = lax.rem(level + dz, levels)
-        return jnp.logical_and(other >= EARLY, jnp.abs(other - level) > 2)
-
     @pl.when(late)
     def _():
-        for (dy, dz), copy in zip(offsets_b, copies_b):
-            if dz in (3, 4, 5):
-                pl.when(jnp.logical_not(far(dz)))(copy.start)
-            else:
+        for (t, y), copy in zip(places, copies_b):
+            if not (t or y):
+                pl.when(jnp.logical_not(in_column))(copy.start)
+            elif t < EARLY:
                 copy.start()
+        send_b(lambda t: jnp.abs(level - t) < 3 if t >= EARLY else None)
 
     @pl.when(early)
     def _():
-        for (dy, dz), copy in zip(offsets_b, copies_b):
-            if dz in (0, 6, 7):
-                pl.when(level + dz >= (levels if dz else 0))(copy.start)
+        send_b(lambda t: level >= t if t < EARLY else None)
 
         @pl.when(level < EARLY - 1)
         def _():
             pl.semaphore_wait(reply_sem.at[2], 4 * (EARLY - 1 - level))
-
-        for (dy, dz), copy in zip(offsets_b, copies_b):
-            if dz in (1, 2):
-                pl.when(level + dz < EARLY)(copy.start)
+            send_b(lambda t: level < t if t < EARLY else None)
+
         pl.semaphore_wait(reply_sem.at[0], 2)
         y_up.start()
 
@@ -406,9 +445,7 @@
     @pl.when(late)
     def _():
         pl.semaphore_wait(round_sem.at[1], len(along_y) + late_steps)
-        for (dy, dz), copy in zip(offsets_b, copies_b):
-            if dz in (3, 4, 5):
-                pl.when(far(dz))(copy.start)
+        send_b(lambda t: jnp.abs(level - t) > 2 if t >= EARLY else None)
 
     lax.fori_loop(6, 8, planes, 0)
 
@@ -586,31 +623,45 @@
     def _():
         wait_bytes(xhalo.at[:, 1], xs_sem.at[1])
 
-    @pl.when(early)
-    def _():
-        wait_bytes(slots_b.at[pl.ds(0, 4 * EARLY - 1)], ts_sem.at[1])
-        wait_bytes(slots_b.at[pl.ds(0, 4 * (8 - EARLY))], tr_sem.at[2])
-
-    @pl.when(level < EARLY - 1)
-    def _():
-        wait_bytes(slots_b.at[pl.ds(0, 4 * EARLY - 1)], tr_sem.at[1])
-
-    @pl.when(last_early)
-    def _():
-        wait_bytes(slots_b.at[pl.ds(0, 5)], ts_sem.at[2])
-
-    @pl.when(late)
-    def _():
-        wait_bytes(slots_b.at[pl.ds(0, 31)], ts_sem.at[1])
-        wait_bytes(slots_b.at[pl.ds(0, 1)], tr_sem.at[1])
-        wait_bytes(slots_b.at[pl.ds(0, 4 * (8 - EARLY) - 1)], tr_sem.at[2])
-
-    others = jnp.sum(slots_b[1 : 4 * EARLY], axis=0)
-    grand[...] = (
-        slots_b[0]
-        + jnp.where(early, others, 0.0)
-        + jnp.sum(slots_b[4 * EARLY :], axis=0)
-    )
+    not_root = jnp.logical_not(root)
+    skips = jnp.logical_and(in_column, not_root)
+
+    def wait_rows(when, count, sem):
+        @pl.when(when)
+        def _():
+            wait_bytes(slots_b.at[pl.ds(0, count)], sem)
+
+    both = jnp.logical_and
+    sent = jnp.logical_not(skips)
+    wait_rows(both(early, sent), 4 * EARLY - 1, ts_sem.at[1])
+    wait_rows(both(early, skips), 4 * EARLY - 2, ts_sem.at[1])
+    wait_rows(both(late, sent), 31, ts_sem.at[1])
+    wait_rows(both(late, skips), 30, ts_sem.at[1])
+    wait_rows(last_early, 5, ts_sem.at[2])
+
+    @pl.when(not_root)
+    def _():
+        to_root.wait_send()
+
+    wait_rows(both(level < EARLY - 1, not_root), 4 * EARLY - 1, tr_sem.at[1])
+    wait_rows(both(early, not_root), 4 * (8 - EARLY), tr_sem.at[2])
+    wait_rows(late, 1, tr_sem.at[1])
+    wait_rows(late, 4 * (8 - EARLY) - 1, tr_sem.at[2])
+
+    @pl.when(root)
+    def _():
+        slots_d[index] = part[0]
+        wait_bytes(slots_d.at[pl.ds(0, 255)], tr_sem.at[3])
+        grand[...] = jnp.sum(slots_d[...], axis=0)
+
+    @pl.when(not_root)
+    def _():
+        others = jnp.sum(slots_b[1 : 4 * EARLY], axis=0)
+        grand[...] = (
+            slots_b[0]
+            + jnp.where(early, others, 0.0)
+            + jnp.sum(slots_b[4 * EARLY :], axis=0)
+        )
 
 
 def write_out(cells, acc, grand, new_density, new_momentum, new_energy, totals, pair, sem):
@@ -665,6 +716,7 @@
             pltpu.VMEM((3, 1, 128), f32),
             pltpu.VMEM((7, 1, 128), f32),
             pltpu.VMEM((32, 1, 128), f32),
+            pltpu.VMEM((256, 1, 128), f32),
             pltpu.SemaphoreType.DMA((4,)),
             pltpu.SemaphoreType.DMA((3,)),
             pltpu.SemaphoreType.DMA((6,)),
@@ -672,8 +724,8 @@
             pltpu.SemaphoreType.DMA((2,)),
             pltpu.SemaphoreType.DMA((2,)),
             pltpu.SemaphoreType.DMA((2,)),
-            pltpu.SemaphoreType.DMA((3,)),
-            pltpu.SemaphoreType.DMA((3,)),
+            pltpu.SemaphoreType.DMA((4,)),
+            pltpu.SemaphoreType.DMA((4,)),
             pltpu.SemaphoreType.REGULAR((2,)),
             pltpu.SemaphoreType.REGULAR((3,)),
         ],

time: 19.8 us -> 19 us (0.960)
  Pallas kernels: 19.1 us -> 18.1 us
    pallas_call x1, Pallas kernels: 18 us -> 17 us  [shards(): pl.pallas_call(kernel, out_shape=(jax.ShapeDtypeStruct((5, 8, 64, 128), f...]
where the time goes in v7:
time: 19 us; the launch traced here: 18.7 us
  Pallas kernels  18.1 us (95%)
  between operations  0.64 us (3%)
    pallas_call x1, Pallas kernels, shards(): pl.pallas_call(kernel, out_shape=(jax.ShapeDtypeStruct((5, 8, 64, 128), f...  17 us
    pallas_call x1, Pallas kernels, shards(): pl.pallas_call(functools.partial(write_out, cells), out_shape=(jax.ShapeD...  1.07 us

profile of v7, /device:TPU:1, one launch (start us, length us, event | category | flops | bytes accessed | tf_op | source)
XLA Modules:
  0.0 18.7 jit_solution(8562921802520873674)
XLA Ops:
  0.6 17.0 %remap.1 = (f32[5,8,64,128]{3,2,1,0:T(8,128)S(1)}, f32[1,128]{1,0:T(1,128)S(1)}) custom-call(f32[8,64,128]{2,1,0:T(8,128)} %density.1, f32[3,8,64,128]{3,2,1,0:T(8,128)} %momentum.1, f32[8,64,128]{2,1,0:T(8,128)} %energy.1, s32[3,8,64,128]{3,2,1,0:T(8,128)} %displacement.1, s32[6]{0:T(128)} %flags.1), custom_call_target="tpu_custom_call" | custom-call | tf_op jit(solution)/shard_map/remap/pallas_call | solution.py:692
  17.7 1.1 %write_out.1 = (f32[8,64,128]{2,1,0:T(8,128)}, f32[3,8,64,128]{3,2,1,0:T(8,128)}, f32[8,64,128]{2,1,0:T(8,128)}, f32[2]{0:T(128)}) custom-call(f32[5,8,64,128]{3,2,1,0:T(8,128)S(1)} %get-tuple-element.6.acc, f32[1,128]{1,0:T(1,128)S(1)} %get-tuple-element.7.grand), custom_call_target="tpu_custom_call" | custom-call | tf_op jit(solution)/shard_map/write_out/pallas_call | solution.py:737

commit v8 on v7

--- a/solution.py
+++ b/solution.py
@@ -10,6 +10,24 @@
 MESH = pl.DeviceIdType.MESH
 STEP = 1.0 / 256.0
 EARLY = 3
+ROOTS = (
+    (0, 0, 0, 1),
+    (0, 1, 0, 0),
+    (0, 0, 1, 0),
+    (0, 2, 0, 0),
+    (0, 3, 0, 0),
+    (0, 0, 2, 0),
+    (0, 0, 3, 0),
+    (0, 0, 0, 0),
+    (0, 1, 0, 1),
+    (0, 2, 0, 1),
+    (0, 1, 1, 0),
+    (0, 0, 1, 1),
+    (1, 0, 0, 0),
+    (1, 0, 0, 1),
+    (1, 1, 0, 0),
+    (1, 0, 1, 0),
+)
 
 
 def minmod(left_diff, right_diff):
@@ -90,6 +108,8 @@
     level = py * 2 + zl
     levels = 2 * ny
     early = level < EARLY
+    both = jnp.logical_and
+    late = jnp.logical_not(early)
 
     def along_yz(dy, dz):
         chip = lax.rem(level + dz, levels)
@@ -104,8 +124,8 @@
         for dc in range(2)
         if dx or dc
     ]
-    along_y = [along_yz(dy, 0) for dy in (1, 2, 3)]
-    steps = [-2, -1, 1, 2]
+    along_y = [along_yz(dy, 0) for dy in (2, 1, 3)]
+    steps = [-2, 2, -1, 1]
     late_step = [
         jnp.logical_and(level + step >= EARLY, level + step < levels) for step in steps
     ]
@@ -121,6 +141,11 @@
                 greet(sem, along_yz(0, step % 8))
 
     barrier = pltpu.get_barrier_semaphore()
+
+    @pl.when(late)
+    def _():
+        greet_late(barrier)
+
     for peer in stage_a + along_y:
         greet(barrier, peer)
 
@@ -137,25 +162,25 @@
     def _():
         greet(barrier, across)
 
-    in_column = jnp.logical_and(px == 0, core == 1)
-    root = jnp.logical_and(in_column, jnp.logical_and(level == 0, pz < 2))
+    me_y = pz // 4
+    in_column = [both(px == x, core == c) for _, x, _, c in ROOTS]
+    skipped = sum(ok.astype(jnp.int32) for ok in in_column)
+    at_root = [
+        both(ok, both(level == t, me_y == y)) for ok, (t, _, y, _) in zip(in_column, ROOTS)
+    ]
+    root = functools.reduce(jnp.logical_or, at_root)
 
     @pl.when(root)
     def _():
         def greet_group(k, carry):
-            t = lax.rem(k // 4 + EARLY, 8)
-            y = lax.rem(k, 4)
-            z = 4 * y + 2 * lax.rem(t, 2)
+            t = 7 - k // 4
+            z = 4 * lax.rem(k, 4) + 2 * lax.rem(t, 2)
             for x in range(4):
                 for c in range(2):
-                    peer = place(x=x, y=t // 2, z=z + c)
-                    if x or not c:
-                        greet(barrier, peer)
-                    else:
-                        pl.when(t + y > 0)(functools.partial(greet, barrier, peer))
+                    greet(barrier, place(x=x, y=t // 2, z=z + c))
             return carry
 
-        lax.fori_loop(0, 32, greet_group, 0)
+        lax.fori_loop(0, 4 * (8 - EARLY), greet_group, 0)
 
     @pl.when(early)
     def _():
@@ -166,9 +191,6 @@
                 for dy in range(4):
                     greet(barrier, along_yz(dy, dz))
 
-    @pl.when(jnp.logical_not(early))
-    def _():
-        greet_late(barrier)
 
     flag_copy.wait()
     wait_bytes(q.at[pl.ds(0, 2)], load_sem.at[1])
@@ -215,8 +237,7 @@
         len(stage_a)
         + len(along_y)
         + has_across.astype(jnp.int32)
-        + 1
-        - root.astype(jnp.int32)
+        + jnp.where(early, 0, len(ROOTS))
         + jnp.where(early, 4 * level, 4 * EARLY + late_steps)
     )
     pl.semaphore_wait(barrier, greeted)
@@ -237,7 +258,6 @@
     ]
     slot = level * 4 + pz // 4
     arrival = tr_sem.at[jnp.where(early, 1, 2)]
-    me_y = pz // 4
     base_z = pz - 4 * me_y - 2 * zl
     places = [(t, y) for t in range(8) for y in (0, 1, 3, 2)]
     copies_b = [
@@ -256,23 +276,30 @@
             ok = wanted(t)
             if ok is not None:
                 other = jnp.logical_or(level != t, me_y != y)
-                if not (t or y):
-                    other = jnp.logical_and(other, jnp.logical_not(in_column))
                 pl.when(jnp.logical_and(ok, other))(copy.start)
-    index = (px * ny + py) * nz + pz
-    to_root = remote(
-        part.at[0], slots_d.at[index], ts_sem.at[3], tr_sem.at[3], place(x=0, y=0, z=1)
-    )
-
-    @pl.when(jnp.logical_not(root))
-    def _():
-        to_root.start()
+    index = (level - EARLY) * 32 + me_y * 8 + px * 2 + core
+    to_roots = [
+        remote(
+            part.at[0],
+            slots_d.at[index],
+            ts_sem.at[3],
+            tr_sem.at[3],
+            place(x=x, y=t // 2, z=4 * y + 2 * (t % 2) + c),
+        )
+        for t, x, y, c in ROOTS
+    ]
+
+    @pl.when(late)
+    def _():
+        to_roots[0].start()
 
     for copy in copies_a:
         copy.start()
 
-    @pl.when(jnp.logical_not(early))
-    def _():
+    @pl.when(late)
+    def _():
+        for copy in to_roots[1:]:
+            copy.start()
         greet_late(round_sem.at[0])
         for peer in along_y:
             greet(round_sem.at[0], peer)
@@ -403,9 +430,7 @@
             acc[f, x] = (value + (flux - pltpu.roll(flux, 63, 0))) + change_z
         return carry
 
-    lax.fori_loop(0, 3, planes, 0)
-
-    late = jnp.logical_not(early)
+    lax.fori_loop(0, 2, planes, 0)
 
     @pl.when(late)
     def _():
@@ -414,6 +439,8 @@
         for peer in along_y:
             greet(round_sem.at[1], peer)
 
+    lax.fori_loop(2, 3, planes, 0)
+
     wait_bytes(slots_a, tr_sem.at[0])
     group = part[0] + jnp.sum(slots_a[...], axis=0)
     part[1] = group
@@ -422,8 +449,9 @@
     @pl.when(late)
     def _():
         for (t, y), copy in zip(places, copies_b):
-            if not (t or y):
-                pl.when(jnp.logical_not(in_column))(copy.start)
+            skip = [ok for ok, spot in zip(in_column, ROOTS) if spot[0] == t and spot[2] == y]
+            if skip:
+                pl.when(jnp.logical_not(functools.reduce(jnp.logical_or, skip)))(copy.start)
             elif t < EARLY:
                 copy.start()
         send_b(lambda t: jnp.abs(level - t) < 3 if t >= EARLY else None)
@@ -432,22 +460,24 @@
     def _():
         send_b(lambda t: level >= t if t < EARLY else None)
 
-        @pl.when(level < EARLY - 1)
-        def _():
-            pl.semaphore_wait(reply_sem.at[2], 4 * (EARLY - 1 - level))
-            send_b(lambda t: level < t if t < EARLY else None)
-
+    lax.fori_loop(3, 5, planes, 0)
+
+    @pl.when(early)
+    def _():
         pl.semaphore_wait(reply_sem.at[0], 2)
         y_up.start()
 
-    lax.fori_loop(3, 6, planes, 0)
-
     @pl.when(late)
     def _():
         pl.semaphore_wait(round_sem.at[1], len(along_y) + late_steps)
         send_b(lambda t: jnp.abs(level - t) > 2 if t >= EARLY else None)
 
-    lax.fori_loop(6, 8, planes, 0)
+    lax.fori_loop(5, 8, planes, 0)
+
+    @pl.when(level < EARLY - 1)
+    def _():
+        pl.semaphore_wait(reply_sem.at[2], 4 * (EARLY - 1 - level))
+        send_b(lambda t: level < t if t < EARLY else None)
 
     @pl.when(jnp.logical_not(first[1]))
     def _():
@@ -624,44 +654,33 @@
         wait_bytes(xhalo.at[:, 1], xs_sem.at[1])
 
     not_root = jnp.logical_not(root)
-    skips = jnp.logical_and(in_column, not_root)
 
     def wait_rows(when, count, sem):
         @pl.when(when)
         def _():
             wait_bytes(slots_b.at[pl.ds(0, count)], sem)
 
-    both = jnp.logical_and
-    sent = jnp.logical_not(skips)
-    wait_rows(both(early, sent), 4 * EARLY - 1, ts_sem.at[1])
-    wait_rows(both(early, skips), 4 * EARLY - 2, ts_sem.at[1])
-    wait_rows(both(late, sent), 31, ts_sem.at[1])
-    wait_rows(both(late, skips), 30, ts_sem.at[1])
+    wait_rows(early, 4 * EARLY - 1, ts_sem.at[1])
+    columns = [(x, c) for _, x, _, c in ROOTS]
+    for skip in sorted({columns.count((x, c)) for x in range(4) for c in range(2)}):
+        wait_rows(both(late, skipped == skip), 31 - skip, ts_sem.at[1])
     wait_rows(last_early, 5, ts_sem.at[2])
-
-    @pl.when(not_root)
-    def _():
-        to_root.wait_send()
-
-    wait_rows(both(level < EARLY - 1, not_root), 4 * EARLY - 1, tr_sem.at[1])
+    wait_rows(late, len(ROOTS), ts_sem.at[3])
+    wait_rows(level < EARLY - 1, 4 * EARLY - 1, tr_sem.at[1])
     wait_rows(both(early, not_root), 4 * (8 - EARLY), tr_sem.at[2])
     wait_rows(late, 1, tr_sem.at[1])
     wait_rows(late, 4 * (8 - EARLY) - 1, tr_sem.at[2])
+    others = jnp.sum(slots_b[1 : 4 * EARLY], axis=0)
+    near_sum = slots_b[0] + jnp.where(early, others, 0.0)
 
     @pl.when(root)
     def _():
-        slots_d[index] = part[0]
-        wait_bytes(slots_d.at[pl.ds(0, 255)], tr_sem.at[3])
-        grand[...] = jnp.sum(slots_d[...], axis=0)
+        wait_bytes(slots_d, tr_sem.at[3])
+        grand[...] = near_sum + jnp.sum(slots_d[...], axis=0)
 
     @pl.when(not_root)
     def _():
-        others = jnp.sum(slots_b[1 : 4 * EARLY], axis=0)
-        grand[...] = (
-            slots_b[0]
-            + jnp.where(early, others, 0.0)
-            + jnp.sum(slots_b[4 * EARLY :], axis=0)
-        )
+        grand[...] = near_sum + jnp.sum(slots_b[4 * EARLY :], axis=0)
 
 
 def write_out(cells, acc, grand, new_density, new_momentum, new_energy, totals, pair, sem):
@@ -716,7 +735,7 @@
             pltpu.VMEM((3, 1, 128), f32),
             pltpu.VMEM((7, 1, 128), f32),
             pltpu.VMEM((32, 1, 128), f32),
-            pltpu.VMEM((256, 1, 128), f32),
+            pltpu.VMEM((160, 1, 128), f32),
             pltpu.SemaphoreType.DMA((4,)),
             pltpu.SemaphoreType.DMA((3,)),
             pltpu.SemaphoreType.DMA((6,)),

time: 19 us -> 18.8 us (0.989); the launches traced: 18.7 us -> 18.7 us
  no operation moved by 1% of the time
where the time goes in v8:
time: 18.8 us; the launch traced here: 18.7 us
  Pallas kernels  18.1 us (96%)
  between operations  0.64 us (3%)
    pallas_call x1, Pallas kernels, shards(): pl.pallas_call(kernel, out_shape=(jax.ShapeDtypeStruct((5, 8, 64, 128), f...  17 us
    pallas_call x1, Pallas kernels, shards(): pl.pallas_call(functools.partial(write_out, cells), out_shape=(jax.ShapeD...  1.07 us

profile of v8, /device:TPU:1, one launch (start us, length us, event | category | flops | bytes accessed | tf_op | source)
XLA Modules:
  0.0 18.7 jit_solution(3148752397018144125)
XLA Ops:
  0.6 17.0 %remap.1 = (f32[5,8,64,128]{3,2,1,0:T(8,128)S(1)}, f32[1,128]{1,0:T(1,128)S(1)}) custom-call(f32[8,64,128]{2,1,0:T(8,128)} %density.1, f32[3,8,64,128]{3,2,1,0:T(8,128)} %momentum.1, f32[8,64,128]{2,1,0:T(8,128)} %energy.1, s32[3,8,64,128]{3,2,1,0:T(8,128)} %displacement.1, s32[6]{0:T(128)} %flags.1), custom_call_target="tpu_custom_call" | custom-call | tf_op jit(solution)/shard_map/remap/pallas_call | solution.py:711
  17.7 1.1 %write_out.1 = (f32[8,64,128]{2,1,0:T(8,128)}, f32[3,8,64,128]{3,2,1,0:T(8,128)}, f32[8,64,128]{2,1,0:T(8,128)}, f32[2]{0:T(128)}) custom-call(f32[5,8,64,128]{3,2,1,0:T(8,128)S(1)} %get-tuple-element.6.acc, f32[1,128]{1,0:T(1,128)S(1)} %get-tuple-element.7.grand), custom_call_target="tpu_custom_call" | custom-call | tf_op jit(solution)/shard_map/write_out/pallas_call | solution.py:756

commit v9 on v8

--- a/solution.py
+++ b/solution.py
@@ -66,11 +66,9 @@
     xface,
     yup,
     ydown,
-    ylow,
-    yhigh,
+    yin,
     zpack,
-    zlow,
-    zhigh,
+    zin,
     zcorr,
     part,
     slots_a,
@@ -86,7 +84,6 @@
     ts_sem,
     tr_sem,
     round_sem,
-    reply_sem,
 ):
     px, py, pz = lax.axis_index("gx"), lax.axis_index("gy"), lax.axis_index("gz")
     nx, ny, nz = lax.axis_size("gx"), lax.axis_size("gy"), lax.axis_size("gz")
@@ -153,9 +150,8 @@
     flag_copy.start()
     pltpu.make_async_copy(density, q.at[0], load_sem.at[1]).start()
     pltpu.make_async_copy(energy, q.at[1], load_sem.at[1]).start()
-    disp_load = pltpu.make_async_copy(displacement, disp, load_sem.at[2])
-    disp_load.start()
-    momentum_load = pltpu.make_async_copy(momentum, q.at[pl.ds(2, 3)], load_sem.at[3])
+    pltpu.make_async_copy(displacement, disp, load_sem.at[1]).start()
+    momentum_load = pltpu.make_async_copy(momentum, q.at[pl.ds(2, 3)], load_sem.at[2])
     momentum_load.start()
 
     @pl.when(has_across)
@@ -193,8 +189,18 @@
 
 
     flag_copy.wait()
-    wait_bytes(q.at[pl.ds(0, 2)], load_sem.at[1])
-    disp_load.wait()
+    wait_bytes(q, load_sem.at[1])
+
+    def wait_pair(buffer, axis, sem):
+        one = jnp.logical_or(first[axis], final[axis])
+
+        @pl.when(one)
+        def _():
+            wait_bytes(buffer.at[0], sem)
+
+        @pl.when(jnp.logical_not(one))
+        def _():
+            wait_bytes(buffer, sem)
 
     flag_open = [flag[i].astype(jnp.float32) for i in range(6)]
     first = [px == 0, py == 0, pz == 0]
@@ -282,8 +288,8 @@
         remote(
             part.at[0],
             slots_d.at[index],
-            ts_sem.at[3],
-            tr_sem.at[3],
+            ts_sem.at[1],
+            tr_sem.at[2],
             place(x=x, y=t // 2, z=4 * y + 2 * (t % 2) + c),
         )
         for t, x, y, c in ROOTS
@@ -308,7 +314,7 @@
 
         @pl.when(jnp.logical_and(level - back_step >= 0, level - back_step < EARLY))
         def _():
-            greet(reply_sem.at[0], along_yz(0, 8 - back_step))
+            greet(round_sem.at[0], along_yz(0, 8 - back_step))
 
     @pl.when(early)
     def _():
@@ -317,20 +323,20 @@
             @pl.when(target < level)
             def _():
                 for dy in range(4):
-                    greet(reply_sem.at[2], along_yz(dy, lax.rem(levels + target - level, levels)))
+                    greet(round_sem.at[2], along_yz(dy, lax.rem(levels + target - level, levels)))
 
     @pl.when(jnp.logical_not(early))
     def _():
-        greet(reply_sem.at[1], along_yz(0, lax.rem(levels + EARLY - 1 - level, levels)))
+        greet(round_sem.at[1], along_yz(0, lax.rem(levels + EARLY - 1 - level, levels)))
 
     x_next = place(x=lax.rem(px + 1, nx))
     x_prev = place(x=lax.rem(px + nx - 1, nx))
-    face_copy = remote(disp.at[0, 0], xface, xs_sem.at[2], xr_sem.at[5], x_prev)
+    face_copy = remote(disp.at[0, 0], xface, xs_sem.at[1], xr_sem.at[2], x_prev)
     up_copies = [
-        remote(q.at[f, pl.ds(6, 2)], xhalo.at[f, 0], xs_sem.at[0], xr_sem.at[f], x_next) for f in range(5)
+        remote(q.at[f, pl.ds(6, 2)], xhalo.at[f, 0], xs_sem.at[0], xr_sem.at[f // 3], x_next) for f in range(5)
     ]
     down_copies = [
-        remote(q.at[f, pl.ds(0, 2)], xhalo.at[f, 1], xs_sem.at[1], xr_sem.at[f], x_prev)
+        remote(q.at[f, pl.ds(0, 2)], xhalo.at[f, 1], xs_sem.at[0], xr_sem.at[f // 3], x_prev)
         for f in range(5)
     ]
 
@@ -352,10 +358,11 @@
         for r in range(2):
             yup[2 * f + r] = q[f, :, 62 + r, :]
             ydown[2 * f + r] = q[f, :, r, :]
+    yup[10] = jnp.zeros((8, 128), jnp.float32)
     ydown[10] = disp[1, :, 0, :].astype(jnp.float32) * STEP
 
-    y_up = remote(yup, ylow, ys_sem.at[0], yr_sem.at[0], place(y=lax.rem(py + 1, ny)))
-    y_down = remote(ydown, yhigh, ys_sem.at[1], yr_sem.at[1], place(y=lax.rem(py + ny - 1, ny)))
+    y_up = remote(yup, yin.at[0], ys_sem.at[0], yr_sem.at[0], place(y=lax.rem(py + 1, ny)))
+    y_down = remote(ydown, yin.at[1], ys_sem.at[0], yr_sem.at[0], place(y=lax.rem(py + ny - 1, ny)))
 
     @pl.when(jnp.logical_not(first[1]))
     def _():
@@ -385,8 +392,8 @@
     for half in range(2):
         zpack[10 + half] = pack(disp, 2, half) * STEP
 
-    z_up = remote(zpack, zlow, zs_sem.at[0], zr_sem.at[0], place(z=lax.rem(pz + 1, nz)))
-    z_down = remote(zpack, zhigh, zs_sem.at[1], zr_sem.at[1], place(z=lax.rem(pz + nz - 1, nz)))
+    z_up = remote(zpack, zin.at[0], zs_sem.at[0], zr_sem.at[0], place(z=lax.rem(pz + 1, nz)))
+    z_down = remote(zpack, zin.at[1], zs_sem.at[0], zr_sem.at[0], place(z=lax.rem(pz + nz - 1, nz)))
 
     @pl.when(jnp.logical_not(final[2]))
     def _():
@@ -464,7 +471,7 @@
 
     @pl.when(early)
     def _():
-        pl.semaphore_wait(reply_sem.at[0], 2)
+        pl.semaphore_wait(round_sem.at[0], 2)
         y_up.start()
 
     @pl.when(late)
@@ -476,19 +483,13 @@
 
     @pl.when(level < EARLY - 1)
     def _():
-        pl.semaphore_wait(reply_sem.at[2], 4 * (EARLY - 1 - level))
+        pl.semaphore_wait(round_sem.at[2], 4 * (EARLY - 1 - level))
         send_b(lambda t: level < t if t < EARLY else None)
 
-    @pl.when(jnp.logical_not(first[1]))
-    def _():
-        y_up.wait_recv()
-
-    @pl.when(jnp.logical_not(final[1]))
-    def _():
-        y_down.wait_recv()
+    wait_pair(yin, 1, yr_sem.at[0])
 
     v0, v1, v63 = [disp[1, :, r, :].astype(jnp.float32) * STEP for r in (0, 1, 63)]
-    v64 = jnp.where(final[1], v63 * flag_open[3], yhigh[10])
+    v64 = jnp.where(final[1], v63 * flag_open[3], yin[1, 10])
     v0 = v0 * low_scale[1]
 
     def flux_row(v, behind, at, slope_behind, slope_at):
@@ -498,10 +499,10 @@
 
     for f in range(5):
         q0, q1, q2, q61, q62, q63 = [q[f, :, r, :] for r in (0, 1, 2, 61, 62, 63)]
-        lo1 = jnp.where(first[1], q0, ylow[2 * f + 1])
-        lo2 = jnp.where(first[1], q0, ylow[2 * f])
-        hi0 = jnp.where(final[1], q63, yhigh[2 * f])
-        hi1 = jnp.where(final[1], q63, yhigh[2 * f + 1])
+        lo1 = jnp.where(first[1], q0, yin[0, 2 * f + 1])
+        lo2 = jnp.where(first[1], q0, yin[0, 2 * f])
+        hi0 = jnp.where(final[1], q63, yin[1, 2 * f])
+        hi1 = jnp.where(final[1], q63, yin[1, 2 * f + 1])
         s0 = minmod(q0 - lo1, q1 - q0)
         s63 = minmod(q63 - q62, hi0 - q63)
         flux_0 = flux_row(v0, lo1, q0, minmod(lo1 - lo2, q0 - lo1), s0)
@@ -513,13 +514,7 @@
         acc[f, :, 62, :] -= flux_63
         acc[f, :, 63, :] += flux_63 - flux_64
 
-    @pl.when(jnp.logical_not(first[2]))
-    def _():
-        z_up.wait_recv()
-
-    @pl.when(jnp.logical_not(final[2]))
-    def _():
-        z_down.wait_recv()
+    wait_pair(zin, 2, zr_sem.at[0])
 
     def face(four, v):
         behind = back(four)
@@ -533,7 +528,7 @@
     for half in range(2):
         own_v = zpack[10 + half]
         v_low = jnp.where(place4 == 2, own_v * low_scale[2], own_v)
-        v_high = jnp.where(final[2], back(own_v) * flag_open[5], zhigh[10 + half])
+        v_high = jnp.where(final[2], back(own_v) * flag_open[5], zin[1, 10 + half])
         left = jnp.minimum(v_low, 0.0)
         left_w = -0.5 * left * (1.0 + left)
         right = jnp.maximum(ahead(own_v), 0.0)
@@ -543,8 +538,8 @@
             own = zpack[j]
             ghost_low = jnp.where(place4 == 0, pltpu.roll(own, 126, 1), ahead(own))
             ghost_high = jnp.where(place4 == 2, back(own), pltpu.roll(own, 2, 1))
-            low = jnp.where(place4 < 2, jnp.where(first[2], ghost_low, zlow[j]), own)
-            high = jnp.where(place4 < 2, own, jnp.where(final[2], ghost_high, zhigh[j]))
+            low = jnp.where(place4 < 2, jnp.where(first[2], ghost_low, zin[0, j]), own)
+            high = jnp.where(place4 < 2, own, jnp.where(final[2], ghost_high, zin[1, j]))
             slope_low, flux_low = face(low, v_low)
             slope_high, flux_high = face(high, v_high)
             by_left = left_w * jnp.where(place4 == 1, slope_high, slope_low)
@@ -562,7 +557,7 @@
 
     last_early = level == EARLY - 1
     copies_c = [
-        remote(part.at[2], slots_b.at[0], ts_sem.at[2], tr_sem.at[1], along_yz(0, dz))
+        remote(part.at[2], slots_b.at[0], ts_sem.at[1], tr_sem.at[1], along_yz(0, dz))
         for dz in range(1, 6)
     ]
 
@@ -570,7 +565,7 @@
     def _():
         wait_bytes(slots_b.at[pl.ds(0, 4 * EARLY - 1)], tr_sem.at[1])
         part[2] = jnp.sum(slots_b[: 4 * EARLY], axis=0)
-        pl.semaphore_wait(reply_sem.at[1], levels - EARLY)
+        pl.semaphore_wait(round_sem.at[1], levels - EARLY)
         for copy in copies_c:
             copy.start()
 
@@ -593,13 +588,16 @@
     edge_lanes = jnp.logical_or(lane8 < 2, lane8 > 125)
     for f in range(5):
 
-        @pl.when(inner)
-        def _():
-            wait_bytes(xhalo.at[f], xr_sem.at[f])
-
-        @pl.when(jnp.logical_not(inner))
-        def _():
-            wait_bytes(xhalo.at[f, 0], xr_sem.at[f])
+        if f in (0, 3):
+            group = pl.ds(f, 3 - f // 3)
+
+            @pl.when(inner)
+            def _():
+                wait_bytes(xhalo.at[group], xr_sem.at[f // 3])
+
+            @pl.when(jnp.logical_not(inner))
+            def _():
+                wait_bytes(xhalo.at[group, 0], xr_sem.at[f // 3])
 
         def tile(t, carry):
             part_rows = pl.ds(pl.multiple_of(t * 8, 8), 8)
@@ -634,38 +632,29 @@
     def _():
         face_copy.wait_send()
 
-    for copy, there in (
-        (y_up, final[1]),
-        (y_down, first[1]),
-        (z_up, final[2]),
-        (z_down, first[2]),
-    ):
-
-        @pl.when(jnp.logical_not(there))
-        def _():
-            copy.wait_send()
-
-    @pl.when(jnp.logical_not(final[0]))
+    wait_pair(yin, 1, ys_sem.at[0])
+    wait_pair(zin, 2, zs_sem.at[0])
+
+    @pl.when(inner)
+    def _():
+        wait_bytes(xhalo, xs_sem.at[0])
+
+    @pl.when(jnp.logical_not(inner))
     def _():
         wait_bytes(xhalo.at[:, 0], xs_sem.at[0])
-
-    @pl.when(jnp.logical_not(first[0]))
-    def _():
-        wait_bytes(xhalo.at[:, 1], xs_sem.at[1])
 
     not_root = jnp.logical_not(root)
 
     def wait_rows(when, count, sem):
         @pl.when(when)
         def _():
-            wait_bytes(slots_b.at[pl.ds(0, count)], sem)
-
-    wait_rows(early, 4 * EARLY - 1, ts_sem.at[1])
+            wait_bytes(slots_d.at[pl.ds(0, count)], sem)
+
+    wait_rows(level < EARLY - 1, 4 * EARLY - 1, ts_sem.at[1])
+    wait_rows(last_early, 4 * EARLY + 4, ts_sem.at[1])
     columns = [(x, c) for _, x, _, c in ROOTS]
     for skip in sorted({columns.count((x, c)) for x in range(4) for c in range(2)}):
-        wait_rows(both(late, skipped == skip), 31 - skip, ts_sem.at[1])
-    wait_rows(last_early, 5, ts_sem.at[2])
-    wait_rows(late, len(ROOTS), ts_sem.at[3])
+        wait_rows(both(late, skipped == skip), 31 - skip + len(ROOTS), ts_sem.at[1])
     wait_rows(level < EARLY - 1, 4 * EARLY - 1, tr_sem.at[1])
     wait_rows(both(early, not_root), 4 * (8 - EARLY), tr_sem.at[2])
     wait_rows(late, 1, tr_sem.at[1])
@@ -675,7 +664,7 @@
 
     @pl.when(root)
     def _():
-        wait_bytes(slots_d, tr_sem.at[3])
+        wait_bytes(slots_d, tr_sem.at[2])
         grand[...] = near_sum + jnp.sum(slots_d[...], axis=0)
 
     @pl.when(not_root)
@@ -724,28 +713,25 @@
             pltpu.VMEM((9, 64, 128), f32),
             pltpu.VMEM((5, 2, 2, 64, 128), f32),
             pltpu.VMEM((64, 128), i32),
-            pltpu.VMEM((10, 8, 128), f32),
             pltpu.VMEM((11, 8, 128), f32),
-            pltpu.VMEM((10, 8, 128), f32),
             pltpu.VMEM((11, 8, 128), f32),
+            pltpu.VMEM((2, 11, 8, 128), f32),
             pltpu.VMEM((12, 8, 128), f32),
-            pltpu.VMEM((12, 8, 128), f32),
-            pltpu.VMEM((12, 8, 128), f32),
+            pltpu.VMEM((2, 12, 8, 128), f32),
             pltpu.VMEM((10, 8, 128), f32),
             pltpu.VMEM((3, 1, 128), f32),
             pltpu.VMEM((7, 1, 128), f32),
             pltpu.VMEM((32, 1, 128), f32),
             pltpu.VMEM((160, 1, 128), f32),
-            pltpu.SemaphoreType.DMA((4,)),
             pltpu.SemaphoreType.DMA((3,)),
-            pltpu.SemaphoreType.DMA((6,)),
             pltpu.SemaphoreType.DMA((2,)),
+            pltpu.SemaphoreType.DMA((3,)),
+            pltpu.SemaphoreType.DMA((1,)),
+            pltpu.SemaphoreType.DMA((1,)),
+            pltpu.SemaphoreType.DMA((1,)),
+            pltpu.SemaphoreType.DMA((1,)),
             pltpu.SemaphoreType.DMA((2,)),
-            pltpu.SemaphoreType.DMA((2,)),
-            pltpu.SemaphoreType.DMA((2,)),
-            pltpu.SemaphoreType.DMA((4,)),
-            pltpu.SemaphoreType.DMA((4,)),
-            pltpu.SemaphoreType.REGULAR((2,)),
+            pltpu.SemaphoreType.DMA((3,)),
             pltpu.SemaphoreType.REGULAR((3,)),
         ],
         compiler_params=pltpu.CompilerParams(

time: 18.8 us -> 18.7 us (level)
  no operation moved by 1% of the time
where the time goes in v9:
time: 18.7 us; the launch traced here: 18.6 us
  Pallas kernels  18 us (96%)
  between operations  0.64 us (3%)
    pallas_call x1, Pallas kernels, shards(): pl.pallas_call(kernel, out_shape=(jax.ShapeDtypeStruct((5, 8, 64, 128), f...  16.9 us
    pallas_call x1, Pallas kernels, shards(): pl.pallas_call(functools.partial(write_out, cells), out_shape=(jax.ShapeD...  1.07 us

profile of v9, /device:TPU:1, one launch (start us, length us, event | category | flops | bytes accessed | tf_op | source)
XLA Modules:
  0.0 18.6 jit_solution(6901525387864663910)
XLA Ops:
  0.6 16.9 %remap.1 = (f32[5,8,64,128]{3,2,1,0:T(8,128)S(1)}, f32[1,128]{1,0:T(1,128)S(1)}) custom-call(f32[8,64,128]{2,1,0:T(8,128)} %density.1, f32[3,8,64,128]{3,2,1,0:T(8,128)} %momentum.1, f32[8,64,128]{2,1,0:T(8,128)} %energy.1, s32[3,8,64,128]{3,2,1,0:T(8,128)} %displacement.1, s32[6]{0:T(128)} %flags.1), custom_call_target="tpu_custom_call" | custom-call | tf_op jit(solution)/shard_map/remap/pallas_call | solution.py:700
  17.5 1.1 %write_out.1 = (f32[8,64,128]{2,1,0:T(8,128)}, f32[3,8,64,128]{3,2,1,0:T(8,128)}, f32[8,64,128]{2,1,0:T(8,128)}, f32[2]{0:T(128)}) custom-call(f32[5,8,64,128]{3,2,1,0:T(8,128)S(1)} %get-tuple-element.6.acc, f32[1,128]{1,0:T(1,128)S(1)} %get-tuple-element.7.grand), custom_call_target="tpu_custom_call" | custom-call | tf_op jit(solution)/shard_map/write_out/pallas_call | solution.py:742

commit v10 on v9

--- a/solution.py
+++ b/solution.py
@@ -39,6 +39,16 @@
 def half_weight(v):
     size = jnp.abs(v)
     return 0.5 * size * (1.0 - size)
+
+
+def row_sum(rows, start, count):
+    sums = [rows[start + i] for i in range(10)]
+    for i in range(10, count):
+        sums[i % 10] = sums[i % 10] + rows[start + i]
+    while len(sums) > 1:
+        paired = [sums[i] + sums[i + 1] for i in range(0, len(sums) - 1, 2)]
+        sums = paired + sums[len(paired) * 2 :]
+    return sums[0]
 
 
 def back(block):
@@ -137,15 +147,6 @@
             def _():
                 greet(sem, along_yz(0, step % 8))
 
-    barrier = pltpu.get_barrier_semaphore()
-
-    @pl.when(late)
-    def _():
-        greet_late(barrier)
-
-    for peer in stage_a + along_y:
-        greet(barrier, peer)
-
     flag_copy = pltpu.make_async_copy(flags, flag, load_sem.at[0])
     flag_copy.start()
     pltpu.make_async_copy(density, q.at[0], load_sem.at[1]).start()
@@ -154,6 +155,15 @@
     momentum_load = pltpu.make_async_copy(momentum, q.at[pl.ds(2, 3)], load_sem.at[2])
     momentum_load.start()
 
+    barrier = pltpu.get_barrier_semaphore()
+
+    @pl.when(late)
+    def _():
+        greet_late(barrier)
+
+    for peer in stage_a + along_y:
+        greet(barrier, peer)
+
     @pl.when(has_across)
     def _():
         greet(barrier, across)
@@ -237,7 +247,6 @@
         return jnp.where(lane1 < 64, low + pltpu.roll(low, 64, 1), high + pltpu.roll(high, 64, 1))
 
     part[0] = halves(*sums)
-    momentum_load.wait()
 
     greeted = (
         len(stage_a)
@@ -329,6 +338,7 @@
     def _():
         greet(round_sem.at[1], along_yz(0, lax.rem(levels + EARLY - 1 - level, levels)))
 
+    momentum_load.wait()
     x_next = place(x=lax.rem(px + 1, nx))
     x_prev = place(x=lax.rem(px + nx - 1, nx))
     face_copy = remote(disp.at[0, 0], xface, xs_sem.at[1], xr_sem.at[2], x_prev)
@@ -665,11 +675,11 @@
     @pl.when(root)
     def _():
         wait_bytes(slots_d, tr_sem.at[2])
-        grand[...] = near_sum + jnp.sum(slots_d[...], axis=0)
+        grand[...] = near_sum + row_sum(slots_d, 0, 160)
 
     @pl.when(not_root)
     def _():
-        grand[...] = near_sum + jnp.sum(slots_b[4 * EARLY :], axis=0)
+        grand[...] = near_sum + row_sum(slots_b, 4 * EARLY, 4 * (8 - EARLY))
 
 
 def write_out(cells, acc, grand, new_density, new_momentum, new_energy, totals, pair, sem):

time: 18.7 us -> 18.3 us (0.979)
  Pallas kernels: 18 us -> 17.6 us
    pallas_call x1, Pallas kernels: 16.9 us -> 16.5 us  [shards(): pl.pallas_call(kernel, out_shape=(jax.ShapeDtypeStruct((5, 8, 64, 128), f...]
where the time goes in v10:
time: 18.3 us; the launch traced here: 18.2 us
  Pallas kernels  17.6 us (96%)
  between operations  0.64 us (3%)
    pallas_call x1, Pallas kernels, shards(): pl.pallas_call(kernel, out_shape=(jax.ShapeDtypeStruct((5, 8, 64, 128), f...  16.5 us
    pallas_call x1, Pallas kernels, shards(): pl.pallas_call(functools.partial(write_out, cells), out_shape=(jax.ShapeD...  1.07 us

profile of v10, /device:TPU:1, one launch (start us, length us, event | category | flops | bytes accessed | tf_op | source)
XLA Modules:
  0.0 18.2 jit_solution(2782514705152645620)
XLA Ops:
  0.6 16.5 %remap.1 = (f32[5,8,64,128]{3,2,1,0:T(8,128)S(1)}, f32[1,128]{1,0:T(1,128)S(1)}) custom-call(f32[8,64,128]{2,1,0:T(8,128)} %density.1, f32[3,8,64,128]{3,2,1,0:T(8,128)} %momentum.1, f32[8,64,128]{2,1,0:T(8,128)} %energy.1, s32[3,8,64,128]{3,2,1,0:T(8,128)} %displacement.1, s32[6]{0:T(128)} %flags.1), custom_call_target="tpu_custom_call" | custom-call | tf_op jit(solution)/shard_map/remap/pallas_call | solution.py:710
  17.2 1.1 %write_out.1 = (f32[8,64,128]{2,1,0:T(8,128)}, f32[3,8,64,128]{3,2,1,0:T(8,128)}, f32[8,64,128]{2,1,0:T(8,128)}, f32[2]{0:T(128)}) custom-call(f32[5,8,64,128]{3,2,1,0:T(8,128)S(1)} %get-tuple-element.6.acc, f32[1,128]{1,0:T(1,128)S(1)} %get-tuple-element.7.grand), custom_call_target="tpu_custom_call" | custom-call | tf_op jit(solution)/shard_map/write_out/pallas_call | solution.py:752

commit v11 on v10

--- a/solution.py
+++ b/solution.py
@@ -151,7 +151,8 @@
     flag_copy.start()
     pltpu.make_async_copy(density, q.at[0], load_sem.at[1]).start()
     pltpu.make_async_copy(energy, q.at[1], load_sem.at[1]).start()
-    pltpu.make_async_copy(displacement, disp, load_sem.at[1]).start()
+    for a in range(3):
+        pltpu.make_async_copy(displacement.at[a], disp.at[a], load_sem.at[1]).start()
     momentum_load = pltpu.make_async_copy(momentum, q.at[pl.ds(2, 3)], load_sem.at[2])
     momentum_load.start()
 

time: 18.3 us -> 18.4 us (level)
  no operation moved by 1% of the time
where the time goes in v11:
time: 18.4 us; the launch traced here: 18.3 us
  Pallas kernels  17.6 us (96%)
  between operations  0.64 us (3%)
    pallas_call x1, Pallas kernels, shards(): pl.pallas_call(kernel, out_shape=(jax.ShapeDtypeStruct((5, 8, 64, 128), f...  16.5 us
    pallas_call x1, Pallas kernels, shards(): pl.pallas_call(functools.partial(write_out, cells), out_shape=(jax.ShapeD...  1.07 us

profile of v11, /device:TPU:1, one launch (start us, length us, event | category | flops | bytes accessed | tf_op | source)
XLA Modules:
  0.0 18.3 jit_solution(16831435502139625383)
XLA Ops:
  0.6 16.5 %remap.1 = (f32[5,8,64,128]{3,2,1,0:T(8,128)S(1)}, f32[1,128]{1,0:T(1,128)S(1)}) custom-call(f32[8,64,128]{2,1,0:T(8,128)} %density.1, f32[3,8,64,128]{3,2,1,0:T(8,128)} %momentum.1, f32[8,64,128]{2,1,0:T(8,128)} %energy.1, s32[3,8,64,128]{3,2,1,0:T(8,128)} %displacement.1, s32[6]{0:T(128)} %flags.1), custom_call_target="tpu_custom_call" | custom-call | tf_op jit(solution)/shard_map/remap/pallas_call | solution.py:711
  17.2 1.1 %write_out.1 = (f32[8,64,128]{2,1,0:T(8,128)}, f32[3,8,64,128]{3,2,1,0:T(8,128)}, f32[8,64,128]{2,1,0:T(8,128)}, f32[2]{0:T(128)}) custom-call(f32[5,8,64,128]{3,2,1,0:T(8,128)S(1)} %get-tuple-element.6.acc, f32[1,128]{1,0:T(1,128)S(1)} %get-tuple-element.7.grand), custom_call_target="tpu_custom_call" | custom-call | tf_op jit(solution)/shard_map/write_out/pallas_call | solution.py:753

commit v12 on v11

--- a/solution.py
+++ b/solution.py
@@ -149,10 +149,15 @@
 
     flag_copy = pltpu.make_async_copy(flags, flag, load_sem.at[0])
     flag_copy.start()
-    pltpu.make_async_copy(density, q.at[0], load_sem.at[1]).start()
-    pltpu.make_async_copy(energy, q.at[1], load_sem.at[1]).start()
+    halves = [pl.ds(0, 4), pl.ds(4, 4)]
+    for half in halves:
+        pltpu.make_async_copy(density.at[half], q.at[0, half], load_sem.at[1]).start()
+        pltpu.make_async_copy(energy.at[half], q.at[1, half], load_sem.at[1]).start()
     for a in range(3):
-        pltpu.make_async_copy(displacement.at[a], disp.at[a], load_sem.at[1]).start()
+        for half in halves:
+            pltpu.make_async_copy(
+                displacement.at[a, half], disp.at[a, half], load_sem.at[1]
+            ).start()
     momentum_load = pltpu.make_async_copy(momentum, q.at[pl.ds(2, 3)], load_sem.at[2])
     momentum_load.start()
 

time: 18.4 us -> 18.4 us (level)
  no operation moved by 1% of the time
where the time goes in v12:
time: 18.4 us; the launch traced here: 18.3 us
  Pallas kernels  17.7 us (96%)
  between operations  0.64 us (3%)
    pallas_call x1, Pallas kernels, shards(): pl.pallas_call(kernel, out_shape=(jax.ShapeDtypeStruct((5, 8, 64, 128), f...  16.6 us
    pallas_call x1, Pallas kernels, shards(): pl.pallas_call(functools.partial(write_out, cells), out_shape=(jax.ShapeD...  1.07 us

profile of v12, /device:TPU:1, one launch (start us, length us, event | category | flops | bytes accessed | tf_op | source)
XLA Modules:
  0.0 18.3 jit_solution(11066249342594253952)
XLA Ops:
  0.6 16.6 %remap.1 = (f32[5,8,64,128]{3,2,1,0:T(8,128)S(1)}, f32[1,128]{1,0:T(1,128)S(1)}) custom-call(f32[8,64,128]{2,1,0:T(8,128)} %density.1, f32[3,8,64,128]{3,2,1,0:T(8,128)} %momentum.1, f32[8,64,128]{2,1,0:T(8,128)} %energy.1, s32[3,8,64,128]{3,2,1,0:T(8,128)} %displacement.1, s32[6]{0:T(128)} %flags.1), custom_call_target="tpu_custom_call" | custom-call | tf_op jit(solution)/shard_map/remap/pallas_call | solution.py:716
  17.2 1.1 %write_out.1 = (f32[8,64,128]{2,1,0:T(8,128)}, f32[3,8,64,128]{3,2,1,0:T(8,128)}, f32[8,64,128]{2,1,0:T(8,128)}, f32[2]{0:T(128)}) custom-call(f32[5,8,64,128]{3,2,1,0:T(8,128)S(1)} %get-tuple-element.6.acc, f32[1,128]{1,0:T(1,128)S(1)} %get-tuple-element.7.grand), custom_call_target="tpu_custom_call" | custom-call | tf_op jit(solution)/shard_map/write_out/pallas_call | solution.py:758
